TPU v7x, 256 devices: a whole 4x4x8 slice. The times are simulated.
256 devices in a mesh: tmpl: 32 (over x, y, core), grid: 8 (over z).
Axes of the slice: x: 4, y: 4, z: 8, core: 2. Of those that a mesh axis runs over, the one named last changes fastest.
Arguments:
- spectrum: float32 [1024, 64, 64, 128], P('tmpl', 'grid'), may hold values from -12 to 12
Outputs:
- best_scores: float32 [4, 64, 64, 64], P(None, 'grid', 'tmpl')
- coherence: float32 [64, 64, 64], P('grid', 'tmpl')
All inputs are finite; a program needn't handle non-finite values.
Results may differ from a plain program's by a relative error of at most 0.0001.
Values sent between devices are 32-bit elements; how exact they have to be, the bound alone decides.
A program may use at most 128 MiB of HBM per device.

v0:
```python
import math

import jax
import jax.numpy as jnp
from jax import lax
from jax.sharding import Mesh
from jax.sharding import PartitionSpec as P

TOP = 4
TMPL = ("tmpl_0", "tmpl_1", "tmpl_2")


FLOOR = -1e30
SPREAD_FLOOR = 0.25


def copy_for_each(value, axis):
    copies = jnp.broadcast_to(value, (lax.axis_size(axis), *value.shape))
    return lax.all_to_all(copies, axis, split_axis=0, concat_axis=0, tiled=True)


def of_everyone(value, axis):
    everything = copy_for_each(value, axis)
    return jnp.sum(everything, axis=0)


def together(arrays, axis):
    ends = [0]
    for a in arrays:
        ends.append(ends[-1] + a.size)
    running = of_everyone(jnp.concatenate([a.ravel() for a in arrays]), axis)
    return tuple((running[b:e].reshape(a.shape) for a, b, e in zip(arrays, ends, ends[1:])))


def cut_along(value, dim, size):
    dims = value.shape
    tiles = value.reshape(*dims[:dim], size, dims[dim] // size, *dims[dim + 1 :])
    return jnp.moveaxis(tiles, dim, 0)


def laid_out(tiles, dim):
    dims = list(tiles.shape[1:])
    dims[dim] *= tiles.shape[0]
    return jnp.moveaxis(tiles, 0, dim).reshape(dims)


def exchange_in_order(tiles, axes, order):
    dims = [lax.axis_size(a) for a in axes]
    tiles = tiles.reshape(*dims, *tiles.shape[1:])
    for k in order:
        tiles = lax.all_to_all(tiles, axes[k], split_axis=k, concat_axis=k, tiled=True)
    return tiles.reshape(-1, *tiles.shape[len(axes) :])


def exchange_by_chip(value, groups, order, split_dim, concat_dim):
    size = lax.axis_size(groups[0]) * lax.axis_size(groups[1])
    tiles = cut_along(value, split_dim, size)
    return laid_out(exchange_in_order(tiles, groups, order), concat_dim)


def phase_table(length):
    order = jnp.arange(length, dtype=jnp.int32)
    turns = order[:, None] * order[None, :] % length
    angle = turns.astype(jnp.float32) * (2.0 * math.pi / length)
    return jnp.concatenate([jnp.cos(angle), -jnp.sin(angle)], axis=0)


def merge_top(former, latter):
    result = []
    for rank_out in range(len(former)):
        winner = jnp.maximum(former[rank_out], latter[rank_out])
        for rank_in in range(rank_out):
            winner = jnp.maximum(
                winner, jnp.minimum(former[rank_in], latter[rank_out - rank_in - 1])
            )
        result.append(winner)
    return tuple(result)


def fold_levels(leaders, running):
    while leaders[0].shape[0] > 1:
        number = leaders[0].shape[0]
        paired = tuple((value.reshape((number // 2, 2) + value.shape[1:]) for value in leaders))
        leaders = merge_top(
            tuple((value[:, 0] for value in paired)), tuple((value[:, 1] for value in paired))
        )
        folded = running.reshape((number // 2, 2) + running.shape[1:])
        running = folded[:, 0] + folded[:, 1]
    return (tuple((value[0] for value in leaders)), running[0])


def body(spectrum):
    local_tmpl, slab_rows, beta_rows, doubled = spectrum.shape
    points = doubled // 2
    paired_table = jnp.kron(jnp.eye(2, dtype=jnp.float32), phase_table(points))
    flat_rows = slab_rows * beta_rows // 2
    score = jnp.dot(
        spectrum.reshape(local_tmpl * flat_rows, 2 * doubled),
        paired_table,
        precision=lax.Precision.HIGHEST,
        preferred_element_type=jnp.float32,
    )
    score = score.reshape(local_tmpl, flat_rows, doubled)
    cell_count = float(points * points * points)
    sum_plain = jnp.sum(score, axis=(1, 2))
    sum_square = jnp.sum(score * score, axis=(1, 2))
    sum_plain, sum_square = together((sum_plain, sum_square), "grid")
    average = sum_plain / cell_count
    spread = sum_square / cell_count - average * average
    centred = score - average[:, None, None]
    normed = centred / jnp.sqrt(spread + SPREAD_FLOOR)[:, None, None]
    filler = jnp.full_like(normed, FLOOR)
    start = (normed,) + tuple((filler for rank_in in range(TOP - 1)))
    leaders, running = fold_levels(start, normed)
    line = beta_rows * points
    leaders = tuple((value.reshape(slab_rows, line) for value in leaders))
    running = running.reshape(slab_rows, line)
    groups = lax.axis_size(TMPL)
    piece = beta_rows // groups
    received = jax.tree.map(
        lambda part: exchange_by_chip(part, (("tmpl_0", "tmpl_1"), "tmpl_2"), (1, 0), 2, 0),
        tuple((value[None] for value in leaders)) + (running[None],),
    )
    best_parts, total_part = fold_levels(received[:-1], received[-1])
    best_scores = jnp.stack(best_parts, axis=0).reshape(TOP, slab_rows, piece, points)
    coherence = (total_part / math.sqrt(groups * local_tmpl)).reshape(slab_rows, piece, points)
    return (best_scores, coherence)


def solution(mesh):
    finer = Mesh(
        mesh.devices.reshape(4, 4, 2, mesh.shape["grid"]), ("tmpl_0", "tmpl_1", "tmpl_2", "grid")
    )
    placed = (P(TMPL, "grid", None, None),)
    return jax.shard_map(
        body,
        mesh=finer,
        in_specs=placed,
        out_specs=(P(None, "grid", TMPL, None), P("grid", TMPL, None)),
        check_vma=False,
    )
```

profile of v0, /device:TPU:32, one launch (start us, length us, event | category | flops | bytes accessed | tf_op | source)
XLA Modules:
  0.0 141.5 jit_solution(16316048197415630682)
XLA Ops:
  0.8 9.8 %reshape.1342 = f32[8192,256]{1,0:T(8,128)} reshape(f32[32,8,64,128]{3,2,1,0:T(8,128)} %param.1) | data formatting | bytes 16777216 | tf_op jit(solution)/shard_map/reshape | solution.py:98
  10.8 13.9 %multiply_reduce_fusion = (f32[8192]{0:T(1024)S(1)}, f32[128,8192]{1,0:T(8,128)}) fusion(f32[8192,256]{1,0:T(8,128)} %reshape.1342, f32[16,8,2,128]{3,2,1,0:T(2,128)S(1)} %bitcast.299), kind=kOutput, calls=%fused_computation.1 | convolution fusion | flops 3223314432 | bytes 12746752 | tf_op jit(solution)/shard_map/dot_general | solution.py:97
  24.8 2.4 %reduce_sum.31 = f32[8192]{0:T(1024)S(1)} reduce(f32[128,8192]{1,0:T(8,128)} %get-tuple-element.37, f32[]{:T(128)} %constant.25.clone.1), dimensions={0}, to_apply=%region_0.1 | reduce | flops 1040384 | bytes 4227076 | tf_op jit(solution)/shard_map/reduce_sum | solution.py:105
  28.1 8.6 %all-to-all-start = ((f32[8,1,64]{2,1,0:T(1,128)}), f32[8,1,64]{2,1,0:T(1,128)S(1)}, u32[]{:S(2)}, u32[]{:S(2)}) async-start(f32[8,1,64]{2,1,0:T(1,128)} %broadcast_in_dim.6), calls=%async_computation | async-start | bytes 8192 | tf_op jit(solution)/shard_map/all_to_all | solution.py:19
  36.6 6.6 %reshape.1343 = f32[16,2,256,128]{2,1,0,3:T(2,128)} reshape(f32[8192,128]{0,1:T(8,128)} %bitcast.276) | data formatting | bytes 8388608 | tf_op jit(solution)/shard_map/reshape | solution.py:103
  43.2 7.4 %copy.215 = f32[16,2,256,128]{3,2,0,1:T(8,128)} copy(f32[16,2,256,128]{2,1,0,3:T(2,128)} %reshape.1343) | data formatting | bytes 8388608 | tf_op jit(solution)/shard_map/reshape | solution.py:103
  51.0 2.8 %subtract_divide_fusion = f32[16,2,256,128]{3,2,0,1:T(8,128)S(1)} fusion(f32[16,2,256,128]{3,2,0,1:T(8,128)} %copy.215, f32[16,2]{0,1:T(2,128)S(1)} %copy.216, f32[16,2]{0,1:T(2,128)S(1)} %copy.214), kind=kLoop, calls=%fused_computation | loop fusion | flops 2097152 | bytes 8388864 | tf_op jit(solution)/shard_map/div | solution.py:111
  53.8 1.3 slice_add_fusion
  55.4 0.7 copy.258
  56.1 0.8 minimum_maximum_fusion.3
  57.8 0.7 copy.250
  58.5 3.4 %all-to-all-start.9 = ((f32[16,2,1,8,128]{4,3,0,2,1:T(8,128)}), f32[16,2,1,8,128]{4,3,0,2,1:T(8,128)S(1)}, u32[]{:S(2)}, u32[]{:S(2)}) async-start(f32[16,2,1,8,128]{4,3,0,2,1:T(8,128)} %copy.258), calls=%async_computation.9 | async-start | bytes 262144 | tf_op jit(solution)/shard_map/all_to_all | solution.py:51
  62.0 1.4 all-to-all-done.9
  63.3 3.4 %all-to-all-start.7 = ((f32[16,2,1,8,128]{4,3,0,2,1:T(8,128)}), f32[16,2,1,8,128]{4,3,0,2,1:T(8,128)S(1)}, u32[]{:S(2)}, u32[]{:S(2)}) async-start(f32[16,2,1,8,128]{4,3,0,2,1:T(8,128)} %copy.250), calls=%async_computation.7 | async-start | bytes 262144 | tf_op jit(solution)/shard_map/all_to_all | solution.py:51
  66.7 0.7 copy.259
  67.4 0.8 all-to-all-done.7
  68.2 3.8 %all_to_all.56 = f32[16,2,1,8,128]{4,3,0,2,1:T(8,128)S(1)} all-to-all(f32[16,2,1,8,128]{4,3,0,2,1:T(8,128)S(1)} %copy.239), channel_id=1, replica_groups=mesh['tmpl_0'=4,'tmpl_1'=4,'tmpl_2'=2,'grid'=8] {'tmpl_2'}, dimensions={1} | all-to-all | bytes 262144 | tf_op jit(solution)/shard_map/all_to_all | solution.py:51
  72.0 3.8 %all_to_all.57 = f32[16,2,1,8,128]{4,3,0,2,1:T(8,128)S(1)} all-to-all(f32[16,2,1,8,128]{4,3,0,2,1:T(8,128)S(1)} %copy.220), channel_id=1, replica_groups=mesh['tmpl_0'=4,'tmpl_1'=4,'tmpl_2'=2,'grid'=8] {'tmpl_2'}, dimensions={1} | all-to-all | bytes 262144 | tf_op jit(solution)/shard_map/all_to_all | solution.py:51
  75.8 3.8 %all_to_all.58 = f32[16,2,1,8,128]{4,3,0,2,1:T(8,128)S(1)} all-to-all(f32[16,2,1,8,128]{4,3,0,2,1:T(8,128)S(1)} %copy.229), channel_id=1, replica_groups=mesh['tmpl_0'=4,'tmpl_1'=4,'tmpl_2'=2,'grid'=8] {'tmpl_2'}, dimensions={1} | all-to-all | bytes 262144 | tf_op jit(solution)/shard_map/all_to_all | solution.py:51
  79.7 7.0 %all-to-all-start.10 = ((f32[16,2,1,8,128]{4,3,1,2,0:T(8,128)}), f32[16,2,1,8,128]{4,3,1,2,0:T(8,128)S(1)}, u32[]{:S(2)}, u32[]{:S(2)}) async-start(f32[16,2,1,8,128]{4,3,1,2,0:T(8,128)} %copy.259), calls=%async_computation.10 | async-start | bytes 262144 | tf_op jit(solution)/shard_map/all_to_all | solution.py:51
  86.7 0.7 copy.251
  87.4 0.7 copy.240
  89.3 5.2 %all-to-all-done.10 = f32[16,2,1,8,128]{4,3,1,2,0:T(8,128)S(1)} async-done(((f32[16,2,1,8,128]{4,3,1,2,0:T(8,128)}), f32[16,2,1,8,128]{4,3,1,2,0:T(8,128)S(1)}, u32[]{:S(2)}, u32[]{:S(2)}) %all-to-all-start.10) | async-done | bytes 131104 | tf_op jit(solution)/shard_map/all_to_all | solution.py:51
  94.5 3.6 %all-to-all-start.2 = ((f32[16,2,1,8,128]{4,3,1,2,0:T(8,128)}), f32[16,2,1,8,128]{4,3,1,2,0:T(8,128)S(1)}, u32[]{:S(2)}, u32[]{:S(2)}) async-start(f32[16,2,1,8,128]{4,3,1,2,0:T(8,128)} %copy.221), calls=%async_computation.2 | async-start | bytes 262144 | tf_op jit(solution)/shard_map/all_to_all | solution.py:51
  98.2 0.7 div.35
  98.9 7.1 %all-to-all-done.2 = f32[16,2,1,8,128]{4,3,1,2,0:T(8,128)S(1)} async-done(((f32[16,2,1,8,128]{4,3,1,2,0:T(8,128)}), f32[16,2,1,8,128]{4,3,1,2,0:T(8,128)S(1)}, u32[]{:S(2)}, u32[]{:S(2)}) %all-to-all-start.2) | async-done | bytes 131104 | tf_op jit(solution)/shard_map/all_to_all | solution.py:51
  106.0 3.6 %all-to-all-start.8 = ((f32[16,2,1,8,128]{4,3,1,2,0:T(8,128)}), f32[16,2,1,8,128]{4,3,1,2,0:T(8,128)S(1)}, u32[]{:S(2)}, u32[]{:S(2)}) async-start(f32[16,2,1,8,128]{4,3,1,2,0:T(8,128)} %copy.251), calls=%async_computation.8 | async-start | bytes 262144 | tf_op jit(solution)/shard_map/all_to_all | solution.py:51
  109.6 7.8 %all-to-all-done.8 = f32[16,2,1,8,128]{4,3,1,2,0:T(8,128)S(1)} async-done(((f32[16,2,1,8,128]{4,3,1,2,0:T(8,128)}), f32[16,2,1,8,128]{4,3,1,2,0:T(8,128)S(1)}, u32[]{:S(2)}, u32[]{:S(2)}) %all-to-all-start.8) | async-done | bytes 131104 | tf_op jit(solution)/shard_map/all_to_all | solution.py:51
  117.4 3.6 %all-to-all-start.6 = ((f32[16,2,1,8,128]{4,3,1,2,0:T(8,128)}), f32[16,2,1,8,128]{4,3,1,2,0:T(8,128)S(1)}, u32[]{:S(2)}, u32[]{:S(2)}) async-start(f32[16,2,1,8,128]{4,3,1,2,0:T(8,128)} %copy.240), calls=%async_computation.6 | async-start | bytes 262144 | tf_op jit(solution)/shard_map/all_to_all | solution.py:51
  121.1 7.8 %all-to-all-done.6 = f32[16,2,1,8,128]{4,3,1,2,0:T(8,128)S(1)} async-done(((f32[16,2,1,8,128]{4,3,1,2,0:T(8,128)}), f32[16,2,1,8,128]{4,3,1,2,0:T(8,128)S(1)}, u32[]{:S(2)}, u32[]{:S(2)}) %all-to-all-start.6) | async-done | bytes 131104 | tf_op jit(solution)/shard_map/all_to_all | solution.py:51
  128.9 3.6 %all-to-all-start.4 = ((f32[16,2,1,8,128]{4,3,1,2,0:T(8,128)}), f32[16,2,1,8,128]{4,3,1,2,0:T(8,128)S(1)}, u32[]{:S(2)}, u32[]{:S(2)}) async-start(f32[16,2,1,8,128]{4,3,1,2,0:T(8,128)} %copy.230), calls=%async_computation.4 | async-start | bytes 262144 | tf_op jit(solution)/shard_map/all_to_all | solution.py:51
  132.5 7.8 %all-to-all-done.4 = f32[16,2,1,8,128]{4,3,1,2,0:T(8,128)S(1)} async-done(((f32[16,2,1,8,128]{4,3,1,2,0:T(8,128)}), f32[16,2,1,8,128]{4,3,1,2,0:T(8,128)S(1)}, u32[]{:S(2)}, u32[]{:S(2)}) %all-to-all-start.4) | async-done | bytes 131104 | tf_op jit(solution)/shard_map/all_to_all | solution.py:51
  (58 shorter events, 5.3 us)
Async XLA Ops:
  28.1 22.5 %all-to-all-start = ((f32[8,1,64]{2,1,0:T(1,128)}), f32[8,1,64]{2,1,0:T(1,128)S(1)}, u32[]{:S(2)}, u32[]{:S(2)}) async-start(f32[8,1,64]{2,1,0:T(1,128)} %broadcast_in_dim.6), calls=%async_computation | async-start | bytes 8192 | tf_op jit(solution)/shard_map/all_to_all | solution.py:19
  58.5 4.8 %all-to-all-start.9 = ((f32[16,2,1,8,128]{4,3,0,2,1:T(8,128)}), f32[16,2,1,8,128]{4,3,0,2,1:T(8,128)S(1)}, u32[]{:S(2)}, u32[]{:S(2)}) async-start(f32[16,2,1,8,128]{4,3,0,2,1:T(8,128)} %copy.258), calls=%async_computation.9 | async-start | bytes 262144 | tf_op jit(solution)/shard_map/all_to_all | solution.py:51
  63.3 4.8 %all-to-all-start.7 = ((f32[16,2,1,8,128]{4,3,0,2,1:T(8,128)}), f32[16,2,1,8,128]{4,3,0,2,1:T(8,128)S(1)}, u32[]{:S(2)}, u32[]{:S(2)}) async-start(f32[16,2,1,8,128]{4,3,0,2,1:T(8,128)} %copy.250), calls=%async_computation.7 | async-start | bytes 262144 | tf_op jit(solution)/shard_map/all_to_all | solution.py:51
  79.7 14.9 %all-to-all-start.10 = ((f32[16,2,1,8,128]{4,3,1,2,0:T(8,128)}), f32[16,2,1,8,128]{4,3,1,2,0:T(8,128)S(1)}, u32[]{:S(2)}, u32[]{:S(2)}) async-start(f32[16,2,1,8,128]{4,3,1,2,0:T(8,128)} %copy.259), calls=%async_computation.10 | async-start | bytes 262144 | tf_op jit(solution)/shard_map/all_to_all | solution.py:51
  94.5 11.4 %all-to-all-start.2 = ((f32[16,2,1,8,128]{4,3,1,2,0:T(8,128)}), f32[16,2,1,8,128]{4,3,1,2,0:T(8,128)S(1)}, u32[]{:S(2)}, u32[]{:S(2)}) async-start(f32[16,2,1,8,128]{4,3,1,2,0:T(8,128)} %copy.221), calls=%async_computation.2 | async-start | bytes 262144 | tf_op jit(solution)/shard_map/all_to_all | solution.py:51
  106.0 11.4 %all-to-all-start.8 = ((f32[16,2,1,8,128]{4,3,1,2,0:T(8,128)}), f32[16,2,1,8,128]{4,3,1,2,0:T(8,128)S(1)}, u32[]{:S(2)}, u32[]{:S(2)}) async-start(f32[16,2,1,8,128]{4,3,1,2,0:T(8,128)} %copy.251), calls=%async_computation.8 | async-start | bytes 262144 | tf_op jit(solution)/shard_map/all_to_all | solution.py:51
  117.4 11.4 %all-to-all-start.6 = ((f32[16,2,1,8,128]{4,3,1,2,0:T(8,128)}), f32[16,2,1,8,128]{4,3,1,2,0:T(8,128)S(1)}, u32[]{:S(2)}, u32[]{:S(2)}) async-start(f32[16,2,1,8,128]{4,3,1,2,0:T(8,128)} %copy.240), calls=%async_computation.6 | async-start | bytes 262144 | tf_op jit(solution)/shard_map/all_to_all | solution.py:51
  128.9 11.4 %all-to-all-start.4 = ((f32[16,2,1,8,128]{4,3,1,2,0:T(8,128)}), f32[16,2,1,8,128]{4,3,1,2,0:T(8,128)S(1)}, u32[]{:S(2)}, u32[]{:S(2)}) async-start(f32[16,2,1,8,128]{4,3,1,2,0:T(8,128)} %copy.230), calls=%async_computation.4 | async-start | bytes 262144 | tf_op jit(solution)/shard_map/all_to_all | solution.py:51
where the time goes:
time: 143 us; the launch traced here: 141 us
  waiting for transfers between devices  37.9 us (27%)
  starting transfers between devices  36.7 us (26%)
  local copies, waits for them, and re-layouts  30.7 us (21%)
  matrix products  13.9 us (10%)
  blocking collectives  11.5 us (8%)
  other arithmetic  9.76 us (7%)
    all_to_all x7, waiting for transfers between devices, exchange_in_order(): lax.all_to_all(tiles, axes[k], split_axis=k, concat_axis=k, tiled=True)  37.9 us
    all_to_all x7, starting transfers between devices, exchange_in_order(): lax.all_to_all(tiles, axes[k], split_axis=k, concat_axis=k, tiled=True)  28.2 us
    reshape x2, local copies, waits for them, and re-layouts, body(): score = score.reshape(local_tmpl, flat_rows, doubled)  13.9 us
    dot_general x1, matrix products, body(): jnp.dot(spectrum.reshape(local_tmpl * flat_rows, 2 * doubled), paired_tab...  13.9 us
    all_to_all x3, blocking collectives, exchange_in_order(): lax.all_to_all(tiles, axes[k], split_axis=k, concat_axis=k, tiled=True)  11.5 us
    reshape x1, local copies, waits for them, and re-layouts, body(): spectrum.reshape(local_tmpl * flat_rows, 2 * doubled)  9.84 us
    all_to_all x1, starting transfers between devices, copy_for_each(): return lax.all_to_all(copies, axis, split_axis=0, concat_axis=0, tiled=True)  8.57 us
    all_to_all x10, local copies, waits for them, and re-layouts, exchange_in_order(): lax.all_to_all(tiles, axes[k], split_axis=k, concat_axis=k, tiled=True)  3.34 us
  transfers between devices with their start and end apart: 8, of which 7 were waited for; matrix products, arithmetic and copies ran while one was open for 13% of the time, Pallas kernels for 0%

commit v1 on v0

v1 whole, which is shorter than its diff:
```python
import functools
import math

import jax
import jax.numpy as jnp
import numpy as np
from jax import lax
from jax.experimental import pallas as pl
from jax.experimental.pallas import tpu as pltpu
from jax.sharding import PartitionSpec as P

TOP = 4
SPREAD_FLOOR = 0.25
LANES = 128
CHUNK = 2
PARTS = TOP + 1


def phase_table(points):
    order = np.arange(points)
    angle = (order[:, None] * order[None, :] % points) * (2.0 * math.pi / points)
    table = np.concatenate([np.cos(angle), -np.sin(angle)], axis=0).astype(np.float32)
    high = table.astype(jnp.bfloat16)
    low = (table - high.astype(np.float32)).astype(jnp.bfloat16)
    pair = lambda part: np.kron(np.eye(2, dtype=np.float32), part.astype(np.float32))
    half = np.concatenate([pair(high), pair(low)], axis=1)
    return np.concatenate([half, half], axis=0).astype(jnp.bfloat16)


def swap(a, b):
    return jnp.maximum(a, b), jnp.minimum(a, b)


def sort_four(a, b, c, d):
    a, b = swap(a, b)
    c, d = swap(c, d)
    a, c = swap(a, c)
    b, d = swap(b, d)
    b, c = swap(b, c)
    return a, b, c, d


def merge_four(first, second):
    a, b, c, d = (jnp.maximum(first[i], second[3 - i]) for i in range(4))
    a, c = swap(a, c)
    b, d = swap(b, d)
    a, b = swap(a, b)
    c, d = swap(c, d)
    return a, b, c, d


def kernel(
    sizes,
    x_hbm,
    table_hbm,
    out_ref,
    x_buf,
    table,
    score,
    other,
    part_sum,
    part_sq,
    stat,
    scale,
    shift,
    mine,
    got,
    x_sem,
    table_sem,
    pair_send,
    pair_recv,
    stat_send,
    stat_recv,
    list_send,
    list_recv,
):
    nx, ny, nz, local = sizes
    chunks = local // CHUNK
    rows = 8
    lines = nx * 8
    places = (nx // 2) * rows
    piece = PARTS * rows
    count = float((2 * lines) ** 3)

    me = lax.axis_index("tmpl")
    z = lax.axis_index("grid")
    chip = me // 2
    core = lax.rem(me, 2)
    x = chip // ny
    sibling = me + 1 - 2 * core

    def load(k):
        return pltpu.make_async_copy(
            x_hbm.at[pl.ds(k * CHUNK, CHUNK)], x_buf.at[pl.ds(k * CHUNK, CHUNK)], x_sem.at[k]
        )

    load(0).start()
    table_copy = pltpu.make_async_copy(table_hbm, table, table_sem)
    table_copy.start()

    @pl.loop(1, chunks)
    def _(k):
        load(k).start()

    barrier = pltpu.get_barrier_semaphore()
    groups = 2 * nx * ny

    @pl.loop(1, groups)
    def _(k):
        pl.semaphore_signal(barrier, inc=1, device_id={"tmpl": lax.rem(me + k, groups), "grid": z})

    @pl.loop(1, nz)
    def _(k):
        for c in range(2):
            pl.semaphore_signal(
                barrier, inc=1, device_id={"tmpl": 2 * chip + c, "grid": lax.rem(z + k, nz)}
            )

    def pair_copy(k):
        part = pl.ds(k * CHUNK, CHUNK)
        return pltpu.make_async_remote_copy(
            src_ref=score.at[1 - core, part],
            dst_ref=other.at[part],
            send_sem=pair_send.at[k],
            recv_sem=pair_recv.at[k],
            device_id={"tmpl": sibling, "grid": z},
        )

    table_copy.wait()

    @pl.loop(0, chunks)
    def _(k):
        load(k).wait()
        for i in range(CHUNK):
            t = k * CHUNK + i
            operands = []
            lows = []
            for parity in range(2):
                value = x_buf[t, :, pl.ds(parity, lines, stride=2), :].reshape(rows * lines, LANES)
                high = value.astype(jnp.bfloat16)
                operands.append(high)
                lows.append((value - high.astype(jnp.float32)).astype(jnp.bfloat16))
            lhs = jnp.concatenate(operands + lows, axis=1)
            product = jnp.dot(lhs, table[...], preferred_element_type=jnp.float32)
            value = product[:, :LANES] + product[:, LANES:]
            value = value.reshape(rows, nx, 8, LANES)
            for g in range(nx):
                h, q = g // (nx // 2), g % (nx // 2)
                score[h, t, pl.ds(q * rows, rows)] = value[:, g]
            flat = value.reshape(rows * nx, 8, LANES)
            part_sum[pl.ds(t, 1)] = jnp.sum(jnp.sum(flat, axis=0), axis=0, keepdims=True)
            part_sq[pl.ds(t, 1)] = jnp.sum(jnp.sum(flat * flat, axis=0), axis=0, keepdims=True)

    pl.semaphore_wait(barrier, groups - 1 + 2 * (nz - 1))

    lane = lax.broadcasted_iota(jnp.int32, (local, LANES), 1)
    line = lax.broadcasted_iota(jnp.int32, (local, LANES), 0)
    sums = jnp.sum(part_sum[...], axis=1, keepdims=True)
    squares = jnp.sum(part_sq[...], axis=1, keepdims=True)
    spread_out = jnp.where(lane == line, sums, 0.0) + jnp.where(lane == line + 64, squares, 0.0)
    own = core * nz + z
    stat[own] = jnp.sum(spread_out, axis=0, keepdims=True)

    @pl.loop(0, chunks)
    def _(k):
        pair_copy(k).start()

    def stat_copy(slot, c, peer_z):
        return pltpu.make_async_remote_copy(
            src_ref=stat.at[slot],
            dst_ref=stat.at[slot],
            send_sem=stat_send.at[c * nz + peer_z],
            recv_sem=stat_recv.at[slot],
            device_id={"tmpl": 2 * chip + c, "grid": peer_z},
        )

    hops = sorted(range(nz), key=lambda k: -min(k, nz - k))
    for k in hops:
        peer_z = lax.rem(z + k, nz)
        for flip in range(2):
            if k or flip:
                stat_copy(own, core * (1 - flip) + (1 - core) * flip, peer_z).start()
    for k in hops:
        peer_z = lax.rem(z + k, nz)
        for flip in range(2):
            if k or flip:
                c = core * (1 - flip) + (1 - core) * flip
                stat_copy(c * nz + peer_z, c, peer_z).wait_recv()

    for side in range(2):
        c = core * (1 - side) + (1 - core) * side
        row = stat[c * nz]
        for k in range(1, nz):
            row = row + stat[c * nz + k]
        row = jnp.broadcast_to(row, (local, LANES))
        total = jnp.sum(jnp.where(lane == line, row, 0.0), axis=1, keepdims=True)
        square = jnp.sum(jnp.where(lane == line + 64, row, 0.0), axis=1, keepdims=True)
        average = total / count
        spread = square / count - average * average
        factor = 1.0 / jnp.sqrt(spread + SPREAD_FLOOR)
        scale[side] = jnp.broadcast_to(factor, (local, LANES))
        shift[side] = jnp.broadcast_to(-average * factor, (local, LANES))

    @pl.loop(0, chunks)
    def _(k):
        pair_copy(k).wait_recv()

    def list_copy(dest, slot_sem):
        return pltpu.make_async_remote_copy(
            src_ref=mine.at[pl.ds(dest * piece, piece)],
            dst_ref=got.at[pl.ds(chip * piece, piece)],
            send_sem=list_send.at[dest],
            recv_sem=list_recv.at[chip],
            device_id={"tmpl": core * (nx * ny) + dest, "grid": z},
        )

    targets = nx * ny
    block = 4

    for q in range(nx // 2):
        for first in range(0, rows, block):
            where = q * rows + first

            def step(n, carry):
                carry = list(carry)
                t = n * 2
                values = []
                for side in range(2):
                    for j in range(2):
                        a = scale[side, pl.ds(t + j, 1), :]
                        b = shift[side, pl.ds(t + j, 1), :]
                        raw = (
                            score[core, t + j, pl.ds(where, block)]
                            if side == 0
                            else other[t + j, pl.ds(where, block)]
                        )
                        values.append(raw * a + b)
                for p in range(block):
                    four = [v[p] for v in values]
                    best = merge_four(carry[p][:TOP], sort_four(*four))
                    carry[p] = best + (carry[p][TOP] + ((four[0] + four[1]) + (four[2] + four[3])),)
                return tuple(carry)

            low = jnp.full((8, LANES), -jnp.inf, jnp.float32)
            start = tuple((low,) * TOP + (jnp.zeros((8, LANES), jnp.float32),) for _ in range(block))
            result = lax.fori_loop(0, local // 2, step, start)
            for p in range(block):
                for part in range(PARTS):
                    mine[pl.ds(q * 8 * piece + part * rows + first + p, 8, stride=piece), :] = result[p][part]

        @pl.loop(0, 8)
        def _(s):
            dest = q * 8 + s

            @pl.when(core * targets + dest != me)
            def _():
                list_copy(dest, chip).start()

    source_core = x // (nx // 2)

    @pl.when(source_core == core)
    def _():
        got[pl.ds(chip * piece, piece), :] = mine[pl.ds((me - core * targets) * piece, piece), :]

    @pl.loop(0, targets)
    def _(q):
        @pl.when(2 * q + source_core != me)
        def _():
            pltpu.make_async_remote_copy(
                src_ref=mine.at[pl.ds(0, piece)],
                dst_ref=got.at[pl.ds(q * piece, piece)],
                send_sem=list_send.at[0],
                recv_sem=list_recv.at[q],
                device_id={"tmpl": 2 * q + source_core, "grid": z},
            ).wait_recv()

    lists = []
    total = None
    for q in range(targets):
        parts = [got[q * piece + rows * k : q * piece + rows * (k + 1), :] for k in range(PARTS)]
        lists.append(parts[:TOP])
        total = parts[TOP] if total is None else total + parts[TOP]
    while len(lists) > 1:
        lists = [merge_four(a, b) for a, b in zip(lists[::2], lists[1::2])]
    for k in range(TOP):
        out_ref[k] = lists[0][k]
    out_ref[TOP] = total * (1.0 / math.sqrt(2 * targets * local))

    @pl.loop(0, chunks)
    def _(k):
        pair_copy(k).wait_send()

    for k in hops:
        peer_z = lax.rem(z + k, nz)
        for flip in range(2):
            if k or flip:
                stat_copy(own, core * (1 - flip) + (1 - core) * flip, peer_z).wait_send()

    @pl.loop(0, targets)
    def _(dest):
        @pl.when(core * targets + dest != me)
        def _():
            list_copy(dest, chip).wait_send()


def body(sizes, spectrum):
    nx, ny, nz, local = sizes
    points = spectrum.shape[3] // 2
    rows = spectrum.shape[1]
    lines = spectrum.shape[2] // 2
    table = jnp.asarray(phase_table(points))
    places = (nx // 2) * rows
    piece = PARTS * rows
    targets = nx * ny
    dma = pltpu.SemaphoreType.DMA
    out = pl.pallas_call(
        functools.partial(kernel, sizes),
        out_shape=jax.ShapeDtypeStruct((PARTS, rows, LANES), jnp.float32),
        in_specs=[pl.BlockSpec(memory_space=pl.ANY)] * 2,
        out_specs=pl.BlockSpec(memory_space=pltpu.VMEM),
        scratch_shapes=[
            pltpu.VMEM(spectrum.shape, jnp.float32),
            pltpu.VMEM(table.shape, jnp.bfloat16),
            pltpu.VMEM((2, local, places, 8, LANES), jnp.float32),
            pltpu.VMEM((local, places, 8, LANES), jnp.float32),
            pltpu.VMEM((local, LANES), jnp.float32),
            pltpu.VMEM((local, LANES), jnp.float32),
            pltpu.VMEM((2 * nz, 1, LANES), jnp.float32),
            pltpu.VMEM((2, local, LANES), jnp.float32),
            pltpu.VMEM((2, local, LANES), jnp.float32),
            pltpu.VMEM((targets * piece, LANES), jnp.float32),
            pltpu.VMEM((targets * piece, LANES), jnp.float32),
            dma((local // CHUNK,)),
            dma,
            dma((local // CHUNK,)),
            dma((local // CHUNK,)),
            dma((2 * nz,)),
            dma((2 * nz,)),
            dma((targets,)),
            dma((targets,)),
        ],
        compiler_params=pltpu.CompilerParams(
            collective_id=0, has_side_effects=True, vmem_limit_bytes=40 * 1024 * 1024
        ),
    )(spectrum, table)
    out = out.reshape(PARTS, rows, 2, points)
    return out[:TOP], out[TOP]


def build(mesh, nx, ny):
    nz = mesh.shape["grid"]

    def run(spectrum):
        sizes = (nx, ny, nz, spectrum.shape[0] // mesh.shape["tmpl"])
        return jax.shard_map(
            functools.partial(body, sizes),
            mesh=mesh,
            in_specs=(P("tmpl", "grid", None, None),),
            out_specs=(P(None, "grid", "tmpl", None), P("grid", "tmpl", None)),
            check_vma=False,
        )(spectrum)

    return run


def solution(mesh):
    return build(mesh, 4, 4)
```

time: 143 us -> 33.8 us (0.24)
  the two profiles are of different devices: /device:TPU:32 before, /device:TPU:1 now
where the time goes in v1:
time: 33.8 us; the launch traced here: 33.7 us
  Pallas kernels  27.3 us (81%)
  local copies, waits for them, and re-layouts  5.7 us (17%)
  between operations  0.66 us (2%)
    pallas_call x1, Pallas kernels, body(): pl.pallas_call(functools.partial(kernel, sizes), out_shape=jax.ShapeDtype...  27.3 us
    unnamed x4, local copies, waits for them, and re-layouts  4.32 us
    slice x3, local copies, waits for them, and re-layouts, body(): return (out[:TOP], out[TOP])  0.7 us

profile of v1, /device:TPU:1, one launch (start us, length us, event | category | flops | bytes accessed | tf_op | source)
XLA Modules:
  0.0 33.7 jit_solution(178156612489964870)
XLA Ops:
  0.6 0.0 copy-start
  0.6 3.4 %copy-done = f32[32,8,64,128]{3,2,1,0:T(8,128)S(1)} copy-done((f32[32,8,64,128]{3,2,1,0:T(8,128)S(1)}, f32[32,8,64,128]{3,2,1,0:T(8,128)}, u32[]{:S(2)}) %copy-start) | copy-done | bytes 8388632
  4.0 0.0 copy-start.1
  4.0 0.9 %copy-done.1 = bf16[512,256]{1,0:T(8,128)(2,1)S(1)} copy-done((bf16[512,256]{1,0:T(8,128)(2,1)S(1)}, bf16[512,256]{1,0:T(8,128)(2,1)}, u32[]{:S(2)}) %copy-start.1) | copy-done | bytes 262168
  5.0 27.3 %shard_map.41 = f32[5,8,128]{2,1,0:T(8,128)S(1)} custom-call(f32[32,8,64,128]{3,2,1,0:T(8,128)S(1)} %copy-done, bf16[512,256]{1,0:T(8,128)(2,1)S(1)} %copy-done.1), custom_call_target="tpu_custom_call" | custom-call | tf_op jit(solution)/shard_map/pallas_call | solution.py:316
  32.3 0.7 %squeeze.3 = f32[8,2,64]{2,1,0:T(2,128)} reshape(f32[1,8,128]{2,1,0:T(8,128)S(1)} %slice.12) | data formatting | bytes 8192 | tf_op jit(solution)/shard_map/squeeze | solution.py:347
  33.0 0.7 %slice.11 = f32[4,8,2,64]{3,2,1,0:T(2,128)} reshape(f32[4,8,128]{2,1,0:T(8,128)S(1)} %slice.10) | data formatting | bytes 32768 | tf_op jit(solution)/shard_map/slice | solution.py:347
  (2 shorter events, 0.0 us)
Async XLA Ops:
  0.6 3.4 %copy-start = (f32[32,8,64,128]{3,2,1,0:T(8,128)S(1)}, f32[32,8,64,128]{3,2,1,0:T(8,128)}, u32[]{:S(2)}) copy-start(f32[32,8,64,128]{3,2,1,0:T(8,128)} %x_hbm.1) | copy-start | bytes 25165828
  4.0 0.9 %copy-start.1 = (bf16[512,256]{1,0:T(8,128)(2,1)S(1)}, bf16[512,256]{1,0:T(8,128)(2,1)}, u32[]{:S(2)}) copy-start(bf16[512,256]{1,0:T(8,128)(2,1)} %constant.2.clone.table_hbm) | copy-start | bytes 786436

commit v2 on v1

v2 whole, which is shorter than its diff:
```python
import functools
import math

import jax
import jax.numpy as jnp
from jax import lax
from jax.experimental import pallas as pl
from jax.experimental.pallas import tpu as pltpu
from jax.sharding import PartitionSpec as P

TOP = 4
SPREAD_FLOOR = 0.25
LANES = 128
CHUNK = 2
PARTS = TOP + 1
MESH = pl.DeviceIdType.MESH


def groups_of(local):
    return (4, 8, 8, 8, 4) if local == 32 else (local // 2, local // 2)


def fill_table(table, points):
    shape = (2 * points, LANES)
    row = lax.broadcasted_iota(jnp.int32, shape, 0)
    lane = lax.broadcasted_iota(jnp.int32, shape, 1)
    quarter = jnp.where(row >= points, points // 4, 0)
    turns = ((row & (points - 1)) * (lane & (points - 1)) + quarter) & (points - 1)
    turns = jnp.where(turns > points // 2, turns - points, turns)
    value = jnp.cos(turns.astype(jnp.float32) * (2.0 * math.pi / points))
    high = value.astype(jnp.bfloat16).astype(jnp.float32)
    for parity in range(2):
        keep = (lane >= points) == bool(parity)
        rows = pl.ds(parity * 2 * points, 2 * points)
        table[rows, 0:LANES] = jnp.where(keep, high, 0.0).astype(jnp.bfloat16)
        table[rows, LANES:] = jnp.where(keep, value - high, 0.0).astype(jnp.bfloat16)


def swap(a, b):
    return jnp.maximum(a, b), jnp.minimum(a, b)


def sort_four(a, b, c, d):
    a, b = swap(a, b)
    c, d = swap(c, d)
    a, c = swap(a, c)
    b, d = swap(b, d)
    b, c = swap(b, c)
    return a, b, c, d


def merge_four(first, second):
    a, b, c, d = (jnp.maximum(first[i], second[3 - i]) for i in range(4))
    a, c = swap(a, c)
    b, d = swap(b, d)
    a, b = swap(a, b)
    c, d = swap(c, d)
    return a, b, c, d


def kernel(
    sizes,
    x_hbm,
    out_ref,
    x_buf,
    table,
    score,
    other,
    part_sum,
    part_sq,
    stat,
    scale,
    shift,
    kept,
    mine,
    got,
    x_sem,
    pair_send,
    pair_recv,
    stat_send,
    stat_recv,
    list_send,
    list_recv,
):
    nx, ny, nz, local = sizes
    chunks = local // CHUNK
    rows = 8
    lines = nx * 8
    piece = PARTS * rows
    targets = nx * ny
    count = float((2 * lines) ** 3)
    sizes_of = groups_of(local)
    groups = len(sizes_of)
    starts = [sum(sizes_of[:g]) for g in range(groups)]
    slots = 2 * nz

    me = lax.axis_index("tmpl")
    z = lax.axis_index("grid")
    chip = me // 2
    core = lax.rem(me, 2)
    x = chip // ny
    y = lax.rem(chip, ny)
    sibling = me + 1 - 2 * core
    plane = 2 * targets
    own = core * nz + z

    def load(k):
        return pltpu.make_async_copy(
            x_hbm.at[pl.ds(k * CHUNK, CHUNK)], x_buf.at[pl.ds(k * CHUNK, CHUNK)], x_sem.at[k]
        )

    @pl.loop(0, chunks)
    def _(k):
        load(k).start()

    barrier = pltpu.get_barrier_semaphore()

    @pl.loop(1, nz)
    def _(k):
        for c in range(2):
            peer = {"tmpl": 2 * chip + c, "grid": lax.rem(z + k, nz)}
            pl.semaphore_signal(barrier, inc=1, device_id=peer, device_id_type=MESH)

    @pl.loop(1, plane)
    def _(k):
        peer = {"tmpl": lax.rem(me + k, plane), "grid": z}
        pl.semaphore_signal(barrier, inc=1, device_id=peer, device_id_type=MESH)

    fill_table(table, x_hbm.shape[3] // 2)

    def pair_copy(g):
        part = pl.ds(starts[g], sizes_of[g])
        return pltpu.make_async_remote_copy(
            src_ref=score.at[1 - core, part],
            dst_ref=other.at[part],
            send_sem=pair_send.at[g],
            recv_sem=pair_recv.at[g],
            device_id={"tmpl": sibling, "grid": z},
            device_id_type=MESH,
        )

    def transform(g):
        weights = table[...]
        for t in range(starts[g], starts[g] + sizes_of[g]):
            if t % CHUNK == 0:
                load(t // CHUNK).wait()
        for t in range(starts[g], starts[g] + sizes_of[g]):
            highs = []
            lows = []
            for parity in range(2):
                value = x_buf[t, :, pl.ds(parity, lines, stride=2), :].reshape(rows * lines, LANES)
                high = value.astype(jnp.bfloat16)
                highs.append(high)
                lows.append((value - high.astype(jnp.float32)).astype(jnp.bfloat16))
            product = jnp.dot(
                jnp.concatenate(highs, axis=1), weights, preferred_element_type=jnp.float32
            ) + jnp.dot(jnp.concatenate(lows, axis=1), weights, preferred_element_type=jnp.float32)
            value = product[:, :LANES] + product[:, LANES:]
            value = value.reshape(rows, nx, 8, LANES)
            for b in range(nx):
                h, q = b // (nx // 2), b % (nx // 2)
                score[h, t, pl.ds(q * rows, rows)] = value[:, b]
            flat = value.reshape(rows * nx, 8, LANES)
            part_sum[pl.ds(t, 1)] = jnp.sum(jnp.sum(flat, axis=0), axis=0, keepdims=True)
            part_sq[pl.ds(t, 1)] = jnp.sum(jnp.sum(flat * flat, axis=0), axis=0, keepdims=True)

    def masks(n):
        lane = lax.broadcasted_iota(jnp.int32, (n, LANES), 1)
        line = lax.broadcasted_iota(jnp.int32, (n, LANES), 0)
        return lane == line, lane == line + LANES // 2

    hops = sorted(range(nz), key=lambda k: -min(k, nz - k))

    def peers():
        for k in hops:
            peer_z = lax.rem(z + k, nz)
            for flip in range(2):
                if k or flip:
                    c = core if flip == 0 else 1 - core
                    yield c, peer_z

    def stat_copy(g, slot, c, peer_z):
        return pltpu.make_async_remote_copy(
            src_ref=stat.at[g * slots + slot],
            dst_ref=stat.at[g * slots + slot],
            send_sem=stat_send.at[g * slots + c * nz + peer_z],
            recv_sem=stat_recv.at[g * slots + slot],
            device_id={"tmpl": 2 * chip + c, "grid": peer_z},
            device_id_type=MESH,
        )

    def share_stats(g):
        part = pl.ds(starts[g], sizes_of[g])
        first, second = masks(sizes_of[g])
        sums = jnp.sum(part_sum[part], axis=1, keepdims=True)
        squares = jnp.sum(part_sq[part], axis=1, keepdims=True)
        line = jnp.where(first, sums, 0.0) + jnp.where(second, squares, 0.0)
        stat[g * slots + own] = jnp.sum(line, axis=0, keepdims=True)
        for c, peer_z in peers():
            stat_copy(g, own, c, peer_z).start()

    def norms(g):
        for c, peer_z in peers():
            stat_copy(g, c * nz + peer_z, c, peer_z).wait_recv()
        part = pl.ds(starts[g], sizes_of[g])
        n = sizes_of[g]
        first, second = masks(n)
        for side in range(2):
            c = core if side == 0 else 1 - core
            line = stat[g * slots + c * nz]
            for k in range(1, nz):
                line = line + stat[g * slots + c * nz + k]
            line = jnp.broadcast_to(line, (n, LANES))
            total = jnp.sum(jnp.where(first, line, 0.0), axis=1, keepdims=True)
            square = jnp.sum(jnp.where(second, line, 0.0), axis=1, keepdims=True)
            average = total / count
            spread = square / count - average * average
            factor = 1.0 / jnp.sqrt(spread + SPREAD_FLOOR)
            scale[side, part] = jnp.broadcast_to(factor, (n, LANES))
            shift[side, part] = jnp.broadcast_to(-average * factor, (n, LANES))

    block = 4
    blocks = (nx // 2) * rows // block

    def best_of(g, where):
        carry = None
        if g:
            carry = [tuple(kept[where + p, k] for k in range(PARTS)) for p in range(block)]
        for t in range(starts[g], starts[g] + sizes_of[g], 2):
            values = []
            for side in range(2):
                for j in range(2):
                    a = scale[side, pl.ds(t + j, 1), :]
                    b = shift[side, pl.ds(t + j, 1), :]
                    at = pl.ds(where, block)
                    raw = score[core, t + j, at] if side == 0 else other[t + j, at]
                    values.append(raw * a + b)
            after = []
            for p in range(block):
                four = [v[p] for v in values]
                best = sort_four(*four)
                total = (four[0] + four[1]) + (four[2] + four[3])
                if carry is not None:
                    best = merge_four(carry[p][:TOP], best)
                    total = carry[p][TOP] + total
                after.append(tuple(best) + (total,))
            carry = after
        return carry

    def list_copy(dest):
        return pltpu.make_async_remote_copy(
            src_ref=mine.at[pl.ds(dest * piece, piece)],
            dst_ref=got.at[pl.ds(chip * piece, piece)],
            send_sem=list_send.at[dest],
            recv_sem=list_recv.at[chip],
            device_id={"tmpl": core * targets + dest, "grid": z},
            device_id_type=MESH,
        )

    waited = max(0, groups - 2)
    for g in range(groups):
        if g == waited:
            pl.semaphore_wait(barrier, plane - 1 + 2 * (nz - 1))
            for before in range(g):
                share_stats(before)
        transform(g)
        if g >= waited:
            share_stats(g)
    for g in range(groups):
        pair_copy(g).start()

    for g in range(groups):
        norms(g)
        pair_copy(g).wait_recv()
        if g < groups - 1:

            @pl.loop(0, blocks)
            def _(n):
                where = n * block
                for p, parts in enumerate(best_of(g, where)):
                    for k in range(PARTS):
                        kept[where + p, k] = parts[k]

        else:
            for q in range(nx // 2):
                for low in range(0, rows, block):
                    for p, parts in enumerate(best_of(g, q * rows + low)):
                        for k in range(PARTS):
                            at = q * 8 * piece + k * rows + low + p
                            mine[pl.ds(at, 8, stride=piece), :] = parts[k]
                for k in (2, 1, 3, 0) if ny == 4 else range(ny):
                    for c in range(2):
                        dest = q * 8 + 2 * lax.rem(y + k, ny) + c

                        @pl.when(core * targets + dest != me)
                        def _():
                            list_copy(dest).start()

    source_core = x // (nx // 2)

    @pl.when(source_core == core)
    def _():
        got[pl.ds(chip * piece, piece), :] = mine[pl.ds((me - core * targets) * piece, piece), :]

    @pl.loop(0, targets)
    def _(q):
        @pl.when(2 * q + source_core != me)
        def _():
            pltpu.make_async_remote_copy(
                src_ref=mine.at[pl.ds(0, piece)],
                dst_ref=got.at[pl.ds(q * piece, piece)],
                send_sem=list_send.at[0],
                recv_sem=list_recv.at[q],
                device_id={"tmpl": 2 * q + source_core, "grid": z},
                device_id_type=MESH,
            ).wait_recv()

    lists = []
    total = None
    for q in range(targets):
        parts = [got[q * piece + rows * k : q * piece + rows * (k + 1), :] for k in range(PARTS)]
        lists.append(parts[:TOP])
        total = parts[TOP] if total is None else total + parts[TOP]
    while len(lists) > 1:
        lists = [merge_four(a, b) for a, b in zip(lists[::2], lists[1::2])]
    for k in range(TOP):
        out_ref[k] = lists[0][k]
    out_ref[TOP] = total * (1.0 / math.sqrt(2 * targets * local))

    for g in range(groups):
        pair_copy(g).wait_send()
        for c, peer_z in peers():
            stat_copy(g, own, c, peer_z).wait_send()

    @pl.loop(0, targets)
    def _(dest):
        @pl.when(core * targets + dest != me)
        def _():
            list_copy(dest).wait_send()


def place_kernel(merged, best_ref, sum_ref):
    half = LANES // 2
    for j in range(2):
        part = slice(j * half, (j + 1) * half)
        for k in range(TOP):
            best_ref[k, :, j, :] = merged[k, :, part]
        sum_ref[:, j, :] = merged[TOP, :, part]


def body(sizes, spectrum):
    nx, ny, nz, local = sizes
    points = spectrum.shape[3] // 2
    rows = spectrum.shape[1]
    places = (nx // 2) * rows
    piece = PARTS * rows
    targets = nx * ny
    groups = len(groups_of(local))
    dma = pltpu.SemaphoreType.DMA
    merged = pl.pallas_call(
        functools.partial(kernel, sizes),
        out_shape=jax.ShapeDtypeStruct((PARTS, rows, LANES), jnp.float32),
        in_specs=[pl.BlockSpec(memory_space=pltpu.HBM)],
        out_specs=pl.BlockSpec(memory_space=pltpu.VMEM),
        scratch_shapes=[
            pltpu.VMEM(spectrum.shape, jnp.float32),
            pltpu.VMEM((4 * points, 2 * LANES), jnp.bfloat16),
            pltpu.VMEM((2, local, places, 8, LANES), jnp.float32),
            pltpu.VMEM((local, places, 8, LANES), jnp.float32),
            pltpu.VMEM((local, LANES), jnp.float32),
            pltpu.VMEM((local, LANES), jnp.float32),
            pltpu.VMEM((groups * 2 * nz, 1, LANES), jnp.float32),
            pltpu.VMEM((2, local, LANES), jnp.float32),
            pltpu.VMEM((2, local, LANES), jnp.float32),
            pltpu.VMEM((places, PARTS, 8, LANES), jnp.float32),
            pltpu.VMEM((targets * piece, LANES), jnp.float32),
            pltpu.VMEM((targets * piece, LANES), jnp.float32),
            dma((local // CHUNK,)),
            dma((groups,)),
            dma((groups,)),
            dma((groups * 2 * nz,)),
            dma((groups * 2 * nz,)),
            dma((targets,)),
            dma((targets,)),
        ],
        compiler_params=pltpu.CompilerParams(
            collective_id=0, has_side_effects=True, vmem_limit_bytes=52 * 1024 * 1024
        ),
    )(spectrum)
    return pl.pallas_call(
        place_kernel,
        out_shape=(
            jax.ShapeDtypeStruct((TOP, rows, 2, points), jnp.float32),
            jax.ShapeDtypeStruct((rows, 2, points), jnp.float32),
        ),
        in_specs=[pl.BlockSpec(memory_space=pltpu.VMEM)],
        out_specs=(pl.BlockSpec(memory_space=pltpu.VMEM),) * 2,
        compiler_params=pltpu.CompilerParams(vmem_limit_bytes=1024 * 1024),
    )(merged)


def build(mesh, nx, ny):
    nz = mesh.shape["grid"]

    def run(spectrum):
        sizes = (nx, ny, nz, spectrum.shape[0] // mesh.shape["tmpl"])
        return jax.shard_map(
            functools.partial(body, sizes),
            mesh=mesh,
            in_specs=(P("tmpl", "grid", None, None),),
            out_specs=(P(None, "grid", "tmpl", None), P("grid", "tmpl", None)),
            check_vma=False,
        )(spectrum)

    return run


def solution(mesh):
    return build(mesh, 4, 4)
```

time: 33.8 us -> 27.9 us (0.83)
  local copies, waits for them, and re-layouts: 5.7 us -> 0 us
    unnamed x4 -> x0, local copies, waits for them, and re-layouts: 4.32 us -> none
    pallas_call x1, Pallas kernels: 27.3 us -> 26.4 us  [body(): pl.pallas_call(functools.partial(kernel, sizes), out_shape=jax.ShapeDtype...]
    pallas_call x0 -> x1, Pallas kernels: none -> 0.72 us  [body(): pl.pallas_call(place_kernel, out_shape=(jax.ShapeDtypeStruct((TOP, rows,...]
    slice x3 -> x0, local copies, waits for them, and re-layouts: 0.7 us -> none  [body(): return (out[:TOP], out[TOP])]
    squeeze x1 -> x0, local copies, waits for them, and re-layouts: 0.68 us -> none  [body(): return (out[:TOP], out[TOP])]
where the time goes in v2:
time: 27.9 us; the launch traced here: 27.8 us
  Pallas kernels  27.1 us (97%)
  between operations  0.64 us (2%)
    pallas_call x1, Pallas kernels, body(): pl.pallas_call(functools.partial(kernel, sizes), out_shape=jax.ShapeDtype...  26.4 us
    pallas_call x1, Pallas kernels, body(): pl.pallas_call(place_kernel, out_shape=(jax.ShapeDtypeStruct((TOP, rows,...  0.72 us

profile of v2, /device:TPU:1, one launch (start us, length us, event | category | flops | bytes accessed | tf_op | source)
XLA Modules:
  0.0 27.8 jit_solution(14180301032734572320)
XLA Ops:
  0.6 26.4 %shard_map.30.merged = f32[5,8,128]{2,1,0:T(8,128)S(1)} custom-call(f32[32,8,64,128]{3,2,1,0:T(8,128)} %x_hbm.1), custom_call_target="tpu_custom_call" | custom-call | tf_op jit(solution)/shard_map/pallas_call | solution.py:360
  27.1 0.7 %shard_map.31 = (f32[4,8,2,64]{3,2,1,0:T(2,128)}, f32[8,2,64]{2,1,0:T(2,128)}) custom-call(f32[5,8,128]{2,1,0:T(8,128)S(1)} %shard_map.30.merged), custom_call_target="tpu_custom_call" | custom-call | tf_op jit(solution)/shard_map/pallas_call | solution.py:390

commit v3 on v2

--- a/solution.py
+++ b/solution.py
@@ -16,8 +16,8 @@
 MESH = pl.DeviceIdType.MESH
 
 
-def groups_of(local):
-    return (4, 8, 8, 8, 4) if local == 32 else (local // 2, local // 2)
+def by_distance(size):
+    return sorted(range(size), key=lambda k: -min(k, size - k))
 
 
 def fill_table(table, points):
@@ -81,6 +81,7 @@
     stat_recv,
     list_send,
     list_recv,
+    products,
 ):
     nx, ny, nz, local = sizes
     chunks = local // CHUNK
@@ -89,9 +90,8 @@
     piece = PARTS * rows
     targets = nx * ny
     count = float((2 * lines) ** 3)
-    sizes_of = groups_of(local)
-    groups = len(sizes_of)
-    starts = [sum(sizes_of[:g]) for g in range(groups)]
+    cut = local * 3 // 4
+    sets = ((0, cut), (cut, local))
     slots = 2 * nz
 
     me = lax.axis_index("tmpl")
@@ -115,21 +115,32 @@
 
     barrier = pltpu.get_barrier_semaphore()
 
-    @pl.loop(1, nz)
-    def _(k):
+    for dx in by_distance(nx):
+        for dy in by_distance(ny):
+            for flip in range(2):
+                if dx or dy or flip:
+                    c = core if flip == 0 else 1 - core
+                    peer = (lax.rem(x + dx, nx) * ny + lax.rem(y + dy, ny)) * 2 + c
+                    pl.semaphore_signal(
+                        barrier,
+                        inc=1,
+                        device_id={"tmpl": peer, "grid": z},
+                        device_id_type=MESH,
+                    )
+    for dz in by_distance(nz):
         for c in range(2):
-            peer = {"tmpl": 2 * chip + c, "grid": lax.rem(z + k, nz)}
-            pl.semaphore_signal(barrier, inc=1, device_id=peer, device_id_type=MESH)
-
-    @pl.loop(1, plane)
-    def _(k):
-        peer = {"tmpl": lax.rem(me + k, plane), "grid": z}
-        pl.semaphore_signal(barrier, inc=1, device_id=peer, device_id_type=MESH)
+            if dz:
+                pl.semaphore_signal(
+                    barrier,
+                    inc=1,
+                    device_id={"tmpl": 2 * chip + c, "grid": lax.rem(z + dz, nz)},
+                    device_id_type=MESH,
+                )
 
     fill_table(table, x_hbm.shape[3] // 2)
 
     def pair_copy(g):
-        part = pl.ds(starts[g], sizes_of[g])
+        part = pl.ds(sets[g][0], sets[g][1] - sets[g][0])
         return pltpu.make_async_remote_copy(
             src_ref=score.at[1 - core, part],
             dst_ref=other.at[part],
@@ -139,40 +150,43 @@
             device_id_type=MESH,
         )
 
-    def transform(g):
-        weights = table[...]
-        for t in range(starts[g], starts[g] + sizes_of[g]):
-            if t % CHUNK == 0:
-                load(t // CHUNK).wait()
-        for t in range(starts[g], starts[g] + sizes_of[g]):
-            highs = []
-            lows = []
+    for unit in range(2):
+        for acc in products[unit]:
+            pltpu.matmul_pop(acc)
+        pltpu.matmul_push_rhs(table[...], staging_register=0, mxu_index=unit)
+
+    def transform(t):
+        for part in range(2):
+            operands = []
             for parity in range(2):
                 value = x_buf[t, :, pl.ds(parity, lines, stride=2), :].reshape(rows * lines, LANES)
                 high = value.astype(jnp.bfloat16)
-                highs.append(high)
-                lows.append((value - high.astype(jnp.float32)).astype(jnp.bfloat16))
-            product = jnp.dot(
-                jnp.concatenate(highs, axis=1), weights, preferred_element_type=jnp.float32
-            ) + jnp.dot(jnp.concatenate(lows, axis=1), weights, preferred_element_type=jnp.float32)
-            value = product[:, :LANES] + product[:, LANES:]
-            value = value.reshape(rows, nx, 8, LANES)
-            for b in range(nx):
-                h, q = b // (nx // 2), b % (nx // 2)
-                score[h, t, pl.ds(q * rows, rows)] = value[:, b]
-            flat = value.reshape(rows * nx, 8, LANES)
-            part_sum[pl.ds(t, 1)] = jnp.sum(jnp.sum(flat, axis=0), axis=0, keepdims=True)
-            part_sq[pl.ds(t, 1)] = jnp.sum(jnp.sum(flat * flat, axis=0), axis=0, keepdims=True)
+                if part:
+                    high = (value - high.astype(jnp.float32)).astype(jnp.bfloat16)
+                operands.append(high)
+            pltpu.matmul_acc_lhs(
+                products[t % 2][t // 2 % 2],
+                jnp.concatenate(operands, axis=1),
+                load_staged_rhs=0 if t < 2 and part == 0 else None,
+            )
+
+    def store(t):
+        product = pltpu.matmul_pop(products[t % 2][t // 2 % 2])
+        value = (product[:, :LANES] + product[:, LANES:]).reshape(rows, nx, 8, LANES)
+        for b in range(nx):
+            h, q = b // (nx // 2), b % (nx // 2)
+            score[h, t, pl.ds(q * rows, rows)] = value[:, b]
+        flat = value.reshape(rows * nx, 8, LANES)
+        part_sum[pl.ds(t, 1)] = jnp.sum(jnp.sum(flat, axis=0), axis=0, keepdims=True)
+        part_sq[pl.ds(t, 1)] = jnp.sum(jnp.sum(flat * flat, axis=0), axis=0, keepdims=True)
 
     def masks(n):
         lane = lax.broadcasted_iota(jnp.int32, (n, LANES), 1)
         line = lax.broadcasted_iota(jnp.int32, (n, LANES), 0)
         return lane == line, lane == line + LANES // 2
 
-    hops = sorted(range(nz), key=lambda k: -min(k, nz - k))
-
     def peers():
-        for k in hops:
+        for k in by_distance(nz):
             peer_z = lax.rem(z + k, nz)
             for flip in range(2):
                 if k or flip:
@@ -183,15 +197,16 @@
         return pltpu.make_async_remote_copy(
             src_ref=stat.at[g * slots + slot],
             dst_ref=stat.at[g * slots + slot],
-            send_sem=stat_send.at[g * slots + c * nz + peer_z],
-            recv_sem=stat_recv.at[g * slots + slot],
+            send_sem=stat_send,
+            recv_sem=stat_recv.at[g],
             device_id={"tmpl": 2 * chip + c, "grid": peer_z},
             device_id_type=MESH,
         )
 
     def share_stats(g):
-        part = pl.ds(starts[g], sizes_of[g])
-        first, second = masks(sizes_of[g])
+        low, high = sets[g]
+        part = pl.ds(low, high - low)
+        first, second = masks(high - low)
         sums = jnp.sum(part_sum[part], axis=1, keepdims=True)
         squares = jnp.sum(part_sq[part], axis=1, keepdims=True)
         line = jnp.where(first, sums, 0.0) + jnp.where(second, squares, 0.0)
@@ -199,11 +214,22 @@
         for c, peer_z in peers():
             stat_copy(g, own, c, peer_z).start()
 
+    def all_stats(g, number):
+        both = stat.at[pl.ds(g * slots, number)]
+        return pltpu.make_async_remote_copy(
+            src_ref=both,
+            dst_ref=both,
+            send_sem=stat_send,
+            recv_sem=stat_recv.at[g],
+            device_id={"tmpl": sibling, "grid": z},
+            device_id_type=MESH,
+        )
+
     def norms(g):
-        for c, peer_z in peers():
-            stat_copy(g, c * nz + peer_z, c, peer_z).wait_recv()
-        part = pl.ds(starts[g], sizes_of[g])
-        n = sizes_of[g]
+        all_stats(g, slots - 1).wait_recv()
+        low, high = sets[g]
+        n = high - low
+        part = pl.ds(low, n)
         first, second = masks(n)
         for side in range(2):
             c = core if side == 0 else 1 - core
@@ -226,7 +252,7 @@
         carry = None
         if g:
             carry = [tuple(kept[where + p, k] for k in range(PARTS)) for p in range(block)]
-        for t in range(starts[g], starts[g] + sizes_of[g], 2):
+        for t in range(sets[g][0], sets[g][1], 2):
             values = []
             for side in range(2):
                 for j in range(2):
@@ -251,28 +277,31 @@
         return pltpu.make_async_remote_copy(
             src_ref=mine.at[pl.ds(dest * piece, piece)],
             dst_ref=got.at[pl.ds(chip * piece, piece)],
-            send_sem=list_send.at[dest],
-            recv_sem=list_recv.at[chip],
+            send_sem=list_send,
+            recv_sem=list_recv,
             device_id={"tmpl": core * targets + dest, "grid": z},
             device_id_type=MESH,
         )
 
-    waited = max(0, groups - 2)
-    for g in range(groups):
-        if g == waited:
+    for k in range(chunks + 1):
+        if k < chunks:
+            load(k).wait()
+            for t in range(k * CHUNK, (k + 1) * CHUNK):
+                transform(t)
+        if k:
+            for t in range((k - 1) * CHUNK, k * CHUNK):
+                store(t)
+        if k * CHUNK == cut:
             pl.semaphore_wait(barrier, plane - 1 + 2 * (nz - 1))
-            for before in range(g):
-                share_stats(before)
-        transform(g)
-        if g >= waited:
-            share_stats(g)
-    for g in range(groups):
+            share_stats(0)
+    share_stats(1)
+    for g in range(2):
         pair_copy(g).start()
 
-    for g in range(groups):
+    for g in range(2):
         norms(g)
         pair_copy(g).wait_recv()
-        if g < groups - 1:
+        if g == 0:
 
             @pl.loop(0, blocks)
             def _(n):
@@ -282,13 +311,15 @@
                         kept[where + p, k] = parts[k]
 
         else:
-            for q in range(nx // 2):
+            half = nx // 2
+            for turn in range(half):
+                q = lax.rem((x + 1) // 2 + 1 + core + turn, 2) if half == 2 else turn
                 for low in range(0, rows, block):
                     for p, parts in enumerate(best_of(g, q * rows + low)):
                         for k in range(PARTS):
-                            at = q * 8 * piece + k * rows + low + p
+                            at = q * (8 * piece) + (k * rows + low + p)
                             mine[pl.ds(at, 8, stride=piece), :] = parts[k]
-                for k in (2, 1, 3, 0) if ny == 4 else range(ny):
+                for k in by_distance(ny):
                     for c in range(2):
                         dest = q * 8 + 2 * lax.rem(y + k, ny) + c
 
@@ -302,18 +333,27 @@
     def _():
         got[pl.ds(chip * piece, piece), :] = mine[pl.ds((me - core * targets) * piece, piece), :]
 
-    @pl.loop(0, targets)
-    def _(q):
-        @pl.when(2 * q + source_core != me)
-        def _():
-            pltpu.make_async_remote_copy(
-                src_ref=mine.at[pl.ds(0, piece)],
-                dst_ref=got.at[pl.ds(q * piece, piece)],
-                send_sem=list_send.at[0],
-                recv_sem=list_recv.at[q],
-                device_id={"tmpl": 2 * q + source_core, "grid": z},
-                device_id_type=MESH,
-            ).wait_recv()
+    all_stats(0, 2 * (slots - 1)).wait_send()
+    for g in range(2):
+        pair_copy(g).wait_send()
+
+    def all_lists(number):
+        return pltpu.make_async_remote_copy(
+            src_ref=mine.at[pl.ds(0, number * piece)],
+            dst_ref=got.at[pl.ds(0, number * piece)],
+            send_sem=list_send,
+            recv_sem=list_recv,
+            device_id={"tmpl": sibling, "grid": z},
+            device_id_type=MESH,
+        )
+
+    @pl.when(source_core == core)
+    def _():
+        all_lists(targets - 1).wait()
+
+    @pl.when(source_core != core)
+    def _():
+        all_lists(targets).wait()
 
     lists = []
     total = None
@@ -327,16 +367,13 @@
         out_ref[k] = lists[0][k]
     out_ref[TOP] = total * (1.0 / math.sqrt(2 * targets * local))
 
-    for g in range(groups):
-        pair_copy(g).wait_send()
-        for c, peer_z in peers():
-            stat_copy(g, own, c, peer_z).wait_send()
-
-    @pl.loop(0, targets)
-    def _(dest):
-        @pl.when(core * targets + dest != me)
-        def _():
-            list_copy(dest).wait_send()
+
+def scoped_kernel(sizes, *refs):
+    def run(*products):
+        kernel(sizes, *refs, (products[:2], products[2:]))
+
+    rows = 2 * LANES
+    pl.run_scoped(run, *(pltpu.ACC(n // 2)((rows, 2 * LANES), jnp.float32) for n in range(4)))
 
 
 def place_kernel(merged, best_ref, sum_ref):
@@ -355,10 +392,9 @@
     places = (nx // 2) * rows
     piece = PARTS * rows
     targets = nx * ny
-    groups = len(groups_of(local))
     dma = pltpu.SemaphoreType.DMA
     merged = pl.pallas_call(
-        functools.partial(kernel, sizes),
+        functools.partial(scoped_kernel, sizes),
         out_shape=jax.ShapeDtypeStruct((PARTS, rows, LANES), jnp.float32),
         in_specs=[pl.BlockSpec(memory_space=pltpu.HBM)],
         out_specs=pl.BlockSpec(memory_space=pltpu.VMEM),
@@ -369,19 +405,19 @@
             pltpu.VMEM((local, places, 8, LANES), jnp.float32),
             pltpu.VMEM((local, LANES), jnp.float32),
             pltpu.VMEM((local, LANES), jnp.float32),
-            pltpu.VMEM((groups * 2 * nz, 1, LANES), jnp.float32),
+            pltpu.VMEM((2 * 2 * nz, 1, LANES), jnp.float32),
             pltpu.VMEM((2, local, LANES), jnp.float32),
             pltpu.VMEM((2, local, LANES), jnp.float32),
             pltpu.VMEM((places, PARTS, 8, LANES), jnp.float32),
             pltpu.VMEM((targets * piece, LANES), jnp.float32),
             pltpu.VMEM((targets * piece, LANES), jnp.float32),
             dma((local // CHUNK,)),
-            dma((groups,)),
-            dma((groups,)),
-            dma((groups * 2 * nz,)),
-            dma((groups * 2 * nz,)),
-            dma((targets,)),
-            dma((targets,)),
+            dma((2,)),
+            dma((2,)),
+            dma,
+            dma((2,)),
+            dma,
+            dma,
         ],
         compiler_params=pltpu.CompilerParams(
             collective_id=0, has_side_effects=True, vmem_limit_bytes=52 * 1024 * 1024

time: 27.9 us -> 25 us (0.90)
  Pallas kernels: 27.1 us -> 24.3 us
    pallas_call x1, Pallas kernels: 26.4 us -> 23.6 us  [body(): pl.pallas_call(functools.partial(scoped_kernel, sizes), out_shape=jax.Sha...]
where the time goes in v3:
time: 25 us
  Pallas kernels  24.3 us (97%)
  between operations  0.64 us (3%)
    pallas_call x1, Pallas kernels, body(): pl.pallas_call(functools.partial(scoped_kernel, sizes), out_shape=jax.Sha...  23.6 us
    pallas_call x1, Pallas kernels, body(): pl.pallas_call(place_kernel, out_shape=(jax.ShapeDtypeStruct((TOP, rows,...  0.72 us

profile of v3, /device:TPU:1, one launch (start us, length us, event | category | flops | bytes accessed | tf_op | source)
XLA Modules:
  0.0 25.0 jit_solution(10027068783013335919)
XLA Ops:
  0.6 23.6 %shard_map.30.merged = f32[5,8,128]{2,1,0:T(8,128)S(1)} custom-call(f32[32,8,64,128]{3,2,1,0:T(8,128)} %refs_0_.1), custom_call_target="tpu_custom_call" | custom-call | tf_op jit(solution)/shard_map/pallas_call | solution.py:396
  24.2 0.7 %shard_map.31 = (f32[4,8,2,64]{3,2,1,0:T(2,128)}, f32[8,2,64]{2,1,0:T(2,128)}) custom-call(f32[5,8,128]{2,1,0:T(8,128)S(1)} %shard_map.30.merged), custom_call_target="tpu_custom_call" | custom-call | tf_op jit(solution)/shard_map/pallas_call | solution.py:426

commit v4 on v3

--- a/solution.py
+++ b/solution.py
@@ -102,6 +102,7 @@
     y = lax.rem(chip, ny)
     sibling = me + 1 - 2 * core
     plane = 2 * targets
+    base = (1 - core) * targets
     own = core * nz + z
 
     def load(k):
@@ -115,6 +116,15 @@
 
     barrier = pltpu.get_barrier_semaphore()
 
+    for dz in by_distance(nz):
+        for c in range(2):
+            if dz:
+                pl.semaphore_signal(
+                    barrier,
+                    inc=1,
+                    device_id={"tmpl": 2 * chip + c, "grid": lax.rem(z + dz, nz)},
+                    device_id_type=MESH,
+                )
     for dx in by_distance(nx):
         for dy in by_distance(ny):
             for flip in range(2):
@@ -127,22 +137,13 @@
                         device_id={"tmpl": peer, "grid": z},
                         device_id_type=MESH,
                     )
-    for dz in by_distance(nz):
-        for c in range(2):
-            if dz:
-                pl.semaphore_signal(
-                    barrier,
-                    inc=1,
-                    device_id={"tmpl": 2 * chip + c, "grid": lax.rem(z + dz, nz)},
-                    device_id_type=MESH,
-                )
 
     fill_table(table, x_hbm.shape[3] // 2)
 
     def pair_copy(g):
         part = pl.ds(sets[g][0], sets[g][1] - sets[g][0])
         return pltpu.make_async_remote_copy(
-            src_ref=score.at[1 - core, part],
+            src_ref=score.at[core, part],
             dst_ref=other.at[part],
             send_sem=pair_send.at[g],
             recv_sem=pair_recv.at[g],
@@ -259,7 +260,7 @@
                     a = scale[side, pl.ds(t + j, 1), :]
                     b = shift[side, pl.ds(t + j, 1), :]
                     at = pl.ds(where, block)
-                    raw = score[core, t + j, at] if side == 0 else other[t + j, at]
+                    raw = score[1 - core, t + j, at] if side == 0 else other[t + j, at]
                     values.append(raw * a + b)
             after = []
             for p in range(block):
@@ -279,7 +280,7 @@
             dst_ref=got.at[pl.ds(chip * piece, piece)],
             send_sem=list_send,
             recv_sem=list_recv,
-            device_id={"tmpl": core * targets + dest, "grid": z},
+            device_id={"tmpl": base + dest, "grid": z},
             device_id_type=MESH,
         )
 
@@ -313,25 +314,31 @@
         else:
             half = nx // 2
             for turn in range(half):
-                q = lax.rem((x + 1) // 2 + 1 + core + turn, 2) if half == 2 else turn
+                q = turn * core + (1 - core) * lax.rem((x + 1) // 2 + turn, 2) if half == 2 else turn
                 for low in range(0, rows, block):
                     for p, parts in enumerate(best_of(g, q * rows + low)):
                         for k in range(PARTS):
                             at = q * (8 * piece) + (k * rows + low + p)
                             mine[pl.ds(at, 8, stride=piece), :] = parts[k]
+                if turn == 0:
+
+                    @pl.when((core == 1) & (me != 1))
+                    def _():
+                        list_copy(1).start()
+
                 for k in by_distance(ny):
                     for c in range(2):
                         dest = q * 8 + 2 * lax.rem(y + k, ny) + c
 
-                        @pl.when(core * targets + dest != me)
+                        @pl.when((base + dest != me) & (base + dest != 1))
                         def _():
                             list_copy(dest).start()
 
-    source_core = x // (nx // 2)
+    source_core = 1 - x // (nx // 2)
 
     @pl.when(source_core == core)
     def _():
-        got[pl.ds(chip * piece, piece), :] = mine[pl.ds((me - core * targets) * piece, piece), :]
+        got[pl.ds(chip * piece, piece), :] = mine[pl.ds((me - base) * piece, piece), :]
 
     all_stats(0, 2 * (slots - 1)).wait_send()
     for g in range(2):

time: 25 us -> 23.6 us (0.944)
  the two profiles are of different devices: /device:TPU:1 before, /device:TPU:7 now
where the time goes in v4:
time: 23.6 us; the launch traced here: 23.5 us
  Pallas kernels  22.9 us (97%)
  between operations  0.64 us (3%)
    pallas_call x1, Pallas kernels, body(): pl.pallas_call(functools.partial(scoped_kernel, sizes), out_shape=jax.Sha...  22.2 us
    pallas_call x1, Pallas kernels, body(): pl.pallas_call(place_kernel, out_shape=(jax.ShapeDtypeStruct((TOP, rows,...  0.72 us

profile of v4, /device:TPU:7, one launch (start us, length us, event | category | flops | bytes accessed | tf_op | source)
XLA Modules:
  0.0 23.5 jit_solution(10686446244538757641)
XLA Ops:
  0.6 22.2 %shard_map.30.merged = f32[5,8,128]{2,1,0:T(8,128)S(1)} custom-call(f32[32,8,64,128]{3,2,1,0:T(8,128)} %refs_0_.1), custom_call_target="tpu_custom_call" | custom-call | tf_op jit(solution)/shard_map/pallas_call | solution.py:403
  22.8 0.7 %shard_map.31 = (f32[4,8,2,64]{3,2,1,0:T(2,128)}, f32[8,2,64]{2,1,0:T(2,128)}) custom-call(f32[5,8,128]{2,1,0:T(8,128)S(1)} %shard_map.30.merged), custom_call_target="tpu_custom_call" | custom-call | tf_op jit(solution)/shard_map/pallas_call | solution.py:433

commit v5 on v4

--- a/solution.py
+++ b/solution.py
@@ -81,6 +81,7 @@
     stat_recv,
     list_send,
     list_recv,
+    plane_sem,
     products,
 ):
     nx, ny, nz, local = sizes
@@ -90,7 +91,7 @@
     piece = PARTS * rows
     targets = nx * ny
     count = float((2 * lines) ** 3)
-    cut = local * 3 // 4
+    cut = local * 5 // 8 // CHUNK * CHUNK
     sets = ((0, cut), (cut, local))
     slots = 2 * nz
 
@@ -101,7 +102,6 @@
     x = chip // ny
     y = lax.rem(chip, ny)
     sibling = me + 1 - 2 * core
-    plane = 2 * targets
     base = (1 - core) * targets
     own = core * nz + z
 
@@ -125,18 +125,24 @@
                     device_id={"tmpl": 2 * chip + c, "grid": lax.rem(z + dz, nz)},
                     device_id_type=MESH,
                 )
-    for dx in by_distance(nx):
-        for dy in by_distance(ny):
-            for flip in range(2):
-                if dx or dy or flip:
-                    c = core if flip == 0 else 1 - core
-                    peer = (lax.rem(x + dx, nx) * ny + lax.rem(y + dy, ny)) * 2 + c
-                    pl.semaphore_signal(
-                        barrier,
-                        inc=1,
-                        device_id={"tmpl": peer, "grid": z},
-                        device_id_type=MESH,
-                    )
+    def near():
+        for c in range(2):
+            for dx in by_distance(nx):
+                if dx:
+                    yield (lax.rem(x + dx, nx) * ny + y) * 2 + c
+            for dy in by_distance(ny):
+                if dy:
+                    yield (x * ny + lax.rem(y + dy, ny)) * 2 + c
+        yield sibling
+
+    def greet(semaphore):
+        for peer in near():
+            pl.semaphore_signal(
+                semaphore, inc=1, device_id={"tmpl": peer, "grid": z}, device_id_type=MESH
+            )
+
+    neighbours = 2 * (nx - 1) + 2 * (ny - 1) + 1
+    greet(barrier)
 
     fill_table(table, x_hbm.shape[3] // 2)
 
@@ -293,15 +299,18 @@
             for t in range((k - 1) * CHUNK, k * CHUNK):
                 store(t)
         if k * CHUNK == cut:
-            pl.semaphore_wait(barrier, plane - 1 + 2 * (nz - 1))
+            pl.semaphore_wait(barrier, neighbours + 2 * (nz - 1))
             share_stats(0)
     share_stats(1)
     for g in range(2):
         pair_copy(g).start()
+    greet(plane_sem)
 
     for g in range(2):
         norms(g)
         pair_copy(g).wait_recv()
+        if g == 1:
+            pl.semaphore_wait(plane_sem, neighbours)
         if g == 0:
 
             @pl.loop(0, blocks)
@@ -320,19 +329,14 @@
                         for k in range(PARTS):
                             at = q * (8 * piece) + (k * rows + low + p)
                             mine[pl.ds(at, 8, stride=piece), :] = parts[k]
-                if turn == 0:
-
-                    @pl.when((core == 1) & (me != 1))
+                order = [(0, 1)] + [(k, c) for k in by_distance(ny) for c in range(2)]
+                for n, (k, c) in enumerate(order):
+                    first = q * 8 + 1
+                    dest = first if n == 0 else q * 8 + 2 * lax.rem(y + k, ny) + c
+
+                    @pl.when((base + dest != me) & ((dest != first) if n else True))
                     def _():
-                        list_copy(1).start()
-
-                for k in by_distance(ny):
-                    for c in range(2):
-                        dest = q * 8 + 2 * lax.rem(y + k, ny) + c
-
-                        @pl.when((base + dest != me) & (base + dest != 1))
-                        def _():
-                            list_copy(dest).start()
+                        list_copy(dest).start()
 
     source_core = 1 - x // (nx // 2)
 
@@ -425,6 +429,7 @@
             dma((2,)),
             dma,
             dma,
+            pltpu.SemaphoreType.REGULAR,
         ],
         compiler_params=pltpu.CompilerParams(
             collective_id=0, has_side_effects=True, vmem_limit_bytes=52 * 1024 * 1024

time: 23.6 us -> 23.2 us (0.983)
  the two profiles are of different devices: /device:TPU:7 before, /device:TPU:6 now
where the time goes in v5:
time: 23.2 us; the launch traced here: 23.1 us
  Pallas kernels  22.5 us (97%)
  between operations  0.64 us (3%)
    pallas_call x1, Pallas kernels, body(): pl.pallas_call(functools.partial(scoped_kernel, sizes), out_shape=jax.Sha...  21.8 us
    pallas_call x1, Pallas kernels, body(): pl.pallas_call(place_kernel, out_shape=(jax.ShapeDtypeStruct((TOP, rows,...  0.72 us

profile of v5, /device:TPU:6, one launch (start us, length us, event | category | flops | bytes accessed | tf_op | source)
XLA Modules:
  0.0 23.1 jit_solution(4449774765352468485)
XLA Ops:
  0.6 21.8 %shard_map.30.merged = f32[5,8,128]{2,1,0:T(8,128)S(1)} custom-call(f32[32,8,64,128]{3,2,1,0:T(8,128)} %refs_0_.1), custom_call_target="tpu_custom_call" | custom-call | tf_op jit(solution)/shard_map/pallas_call | solution.py:407
  22.4 0.7 %shard_map.31 = (f32[4,8,2,64]{3,2,1,0:T(2,128)}, f32[8,2,64]{2,1,0:T(2,128)}) custom-call(f32[5,8,128]{2,1,0:T(8,128)S(1)} %shard_map.30.merged), custom_call_target="tpu_custom_call" | custom-call | tf_op jit(solution)/shard_map/pallas_call | solution.py:438

commit v6 on v5

--- a/solution.py
+++ b/solution.py
@@ -102,7 +102,14 @@
     x = chip // ny
     y = lax.rem(chip, ny)
     sibling = me + 1 - 2 * core
-    base = (1 - core) * targets
+
+    def step_of(slot):
+        return 3 - core + slot * (2 * core - 3)
+
+    def place_of(column):
+        step = lax.rem(column - x + nx, nx)
+        return lax.rem((step + 1) // 2, 2), 1 - step // 2
+
     own = core * nz + z
 
     def load(k):
@@ -149,13 +156,15 @@
     def pair_copy(g):
         part = pl.ds(sets[g][0], sets[g][1] - sets[g][0])
         return pltpu.make_async_remote_copy(
-            src_ref=score.at[core, part],
+            src_ref=score.at[1 - core, part],
             dst_ref=other.at[part],
             send_sem=pair_send.at[g],
             recv_sem=pair_recv.at[g],
             device_id={"tmpl": sibling, "grid": z},
             device_id_type=MESH,
         )
+
+    places_of = [place_of(b) for b in range(nx)]
 
     for unit in range(2):
         for acc in products[unit]:
@@ -181,8 +190,8 @@
         product = pltpu.matmul_pop(products[t % 2][t // 2 % 2])
         value = (product[:, :LANES] + product[:, LANES:]).reshape(rows, nx, 8, LANES)
         for b in range(nx):
-            h, q = b // (nx // 2), b % (nx // 2)
-            score[h, t, pl.ds(q * rows, rows)] = value[:, b]
+            h, slot = places_of[b]
+            score[h, t, pl.ds(slot * rows, rows)] = value[:, b]
         flat = value.reshape(rows * nx, 8, LANES)
         part_sum[pl.ds(t, 1)] = jnp.sum(jnp.sum(flat, axis=0), axis=0, keepdims=True)
         part_sq[pl.ds(t, 1)] = jnp.sum(jnp.sum(flat * flat, axis=0), axis=0, keepdims=True)
@@ -266,7 +275,7 @@
                     a = scale[side, pl.ds(t + j, 1), :]
                     b = shift[side, pl.ds(t + j, 1), :]
                     at = pl.ds(where, block)
-                    raw = score[1 - core, t + j, at] if side == 0 else other[t + j, at]
+                    raw = score[core, t + j, at] if side == 0 else other[t + j, at]
                     values.append(raw * a + b)
             after = []
             for p in range(block):
@@ -280,13 +289,14 @@
             carry = after
         return carry
 
-    def list_copy(dest):
+    def list_copy(slot, line):
+        column = lax.rem(x + step_of(slot), nx)
         return pltpu.make_async_remote_copy(
-            src_ref=mine.at[pl.ds(dest * piece, piece)],
+            src_ref=mine.at[pl.ds((slot * 8 + line) * piece, piece)],
             dst_ref=got.at[pl.ds(chip * piece, piece)],
             send_sem=list_send,
             recv_sem=list_recv,
-            device_id={"tmpl": base + dest, "grid": z},
+            device_id={"tmpl": column * (2 * ny) + line, "grid": z},
             device_id_type=MESH,
         )
 
@@ -321,28 +331,27 @@
                         kept[where + p, k] = parts[k]
 
         else:
-            half = nx // 2
-            for turn in range(half):
-                q = turn * core + (1 - core) * lax.rem((x + 1) // 2 + turn, 2) if half == 2 else turn
+            swap = (1 - core) * (1 - (x + 3) // 4) + core * (x // 3)
+            for turn in range(2):
+                slot = turn + swap * (1 - 2 * turn)
                 for low in range(0, rows, block):
-                    for p, parts in enumerate(best_of(g, q * rows + low)):
+                    for p, parts in enumerate(best_of(g, slot * rows + low)):
                         for k in range(PARTS):
-                            at = q * (8 * piece) + (k * rows + low + p)
+                            at = slot * (8 * piece) + (k * rows + low + p)
                             mine[pl.ds(at, 8, stride=piece), :] = parts[k]
+                own_column = (core == 0) & (slot == 1)
                 order = [(0, 1)] + [(k, c) for k in by_distance(ny) for c in range(2)]
                 for n, (k, c) in enumerate(order):
-                    first = q * 8 + 1
-                    dest = first if n == 0 else q * 8 + 2 * lax.rem(y + k, ny) + c
-
-                    @pl.when((base + dest != me) & ((dest != first) if n else True))
+                    line = 1 if n == 0 else 2 * lax.rem(y + k, ny) + c
+                    here = jnp.logical_not(own_column & (line == 2 * y + core))
+
+                    @pl.when(here & ((line != 1) if n else True))
                     def _():
-                        list_copy(dest).start()
-
-    source_core = 1 - x // (nx // 2)
-
-    @pl.when(source_core == core)
+                        list_copy(slot, line).start()
+
+    @pl.when(core == 0)
     def _():
-        got[pl.ds(chip * piece, piece), :] = mine[pl.ds((me - base) * piece, piece), :]
+        got[pl.ds(chip * piece, piece), :] = mine[pl.ds((8 + 2 * y) * piece, piece), :]
 
     all_stats(0, 2 * (slots - 1)).wait_send()
     for g in range(2):
@@ -358,11 +367,11 @@
             device_id_type=MESH,
         )
 
-    @pl.when(source_core == core)
+    @pl.when(core == 0)
     def _():
         all_lists(targets - 1).wait()
 
-    @pl.when(source_core != core)
+    @pl.when(core == 1)
     def _():
         all_lists(targets).wait()
 

time: 23.2 us -> 23.2 us (level)
  the two profiles are of different devices: /device:TPU:6 before, /device:TPU:1 now
where the time goes in v6:
time: 23.2 us; the launch traced here: 23.1 us
  Pallas kernels  22.4 us (97%)
  between operations  0.64 us (3%)
    pallas_call x1, Pallas kernels, body(): pl.pallas_call(functools.partial(scoped_kernel, sizes), out_shape=jax.Sha...  21.7 us
    pallas_call x1, Pallas kernels, body(): pl.pallas_call(place_kernel, out_shape=(jax.ShapeDtypeStruct((TOP, rows,...  0.72 us

profile of v6, /device:TPU:1, one launch (start us, length us, event | category | flops | bytes accessed | tf_op | source)
XLA Modules:
  0.0 23.1 jit_solution(8371257689735635091)
XLA Ops:
  0.6 21.7 %shard_map.30.merged = f32[5,8,128]{2,1,0:T(8,128)S(1)} custom-call(f32[32,8,64,128]{3,2,1,0:T(8,128)} %refs_0_.1), custom_call_target="tpu_custom_call" | custom-call | tf_op jit(solution)/shard_map/pallas_call | solution.py:416
  22.3 0.7 %shard_map.31 = (f32[4,8,2,64]{3,2,1,0:T(2,128)}, f32[8,2,64]{2,1,0:T(2,128)}) custom-call(f32[5,8,128]{2,1,0:T(8,128)S(1)} %shard_map.30.merged), custom_call_target="tpu_custom_call" | custom-call | tf_op jit(solution)/shard_map/pallas_call | solution.py:447

commit v7 on v6

--- a/solution.py
+++ b/solution.py
@@ -74,7 +74,6 @@
     kept,
     mine,
     got,
-    x_sem,
     pair_send,
     pair_recv,
     stat_send,
@@ -82,7 +81,6 @@
     list_send,
     list_recv,
     plane_sem,
-    products,
 ):
     nx, ny, nz, local = sizes
     chunks = local // CHUNK
@@ -112,26 +110,8 @@
 
     own = core * nz + z
 
-    def load(k):
-        return pltpu.make_async_copy(
-            x_hbm.at[pl.ds(k * CHUNK, CHUNK)], x_buf.at[pl.ds(k * CHUNK, CHUNK)], x_sem.at[k]
-        )
-
-    @pl.loop(0, chunks)
-    def _(k):
-        load(k).start()
-
     barrier = pltpu.get_barrier_semaphore()
 
-    for dz in by_distance(nz):
-        for c in range(2):
-            if dz:
-                pl.semaphore_signal(
-                    barrier,
-                    inc=1,
-                    device_id={"tmpl": 2 * chip + c, "grid": lax.rem(z + dz, nz)},
-                    device_id_type=MESH,
-                )
     def near():
         for c in range(2):
             for dx in by_distance(nx):
@@ -149,52 +129,18 @@
             )
 
     neighbours = 2 * (nx - 1) + 2 * (ny - 1) + 1
-    greet(barrier)
-
-    fill_table(table, x_hbm.shape[3] // 2)
-
     def pair_copy(g):
         part = pl.ds(sets[g][0], sets[g][1] - sets[g][0])
         return pltpu.make_async_remote_copy(
             src_ref=score.at[1 - core, part],
             dst_ref=other.at[part],
-            send_sem=pair_send.at[g],
+            send_sem=pair_send,
             recv_sem=pair_recv.at[g],
             device_id={"tmpl": sibling, "grid": z},
             device_id_type=MESH,
         )
 
     places_of = [place_of(b) for b in range(nx)]
-
-    for unit in range(2):
-        for acc in products[unit]:
-            pltpu.matmul_pop(acc)
-        pltpu.matmul_push_rhs(table[...], staging_register=0, mxu_index=unit)
-
-    def transform(t):
-        for part in range(2):
-            operands = []
-            for parity in range(2):
-                value = x_buf[t, :, pl.ds(parity, lines, stride=2), :].reshape(rows * lines, LANES)
-                high = value.astype(jnp.bfloat16)
-                if part:
-                    high = (value - high.astype(jnp.float32)).astype(jnp.bfloat16)
-                operands.append(high)
-            pltpu.matmul_acc_lhs(
-                products[t % 2][t // 2 % 2],
-                jnp.concatenate(operands, axis=1),
-                load_staged_rhs=0 if t < 2 and part == 0 else None,
-            )
-
-    def store(t):
-        product = pltpu.matmul_pop(products[t % 2][t // 2 % 2])
-        value = (product[:, :LANES] + product[:, LANES:]).reshape(rows, nx, 8, LANES)
-        for b in range(nx):
-            h, slot = places_of[b]
-            score[h, t, pl.ds(slot * rows, rows)] = value[:, b]
-        flat = value.reshape(rows * nx, 8, LANES)
-        part_sum[pl.ds(t, 1)] = jnp.sum(jnp.sum(flat, axis=0), axis=0, keepdims=True)
-        part_sq[pl.ds(t, 1)] = jnp.sum(jnp.sum(flat * flat, axis=0), axis=0, keepdims=True)
 
     def masks(n):
         lane = lax.broadcasted_iota(jnp.int32, (n, LANES), 1)
@@ -300,21 +246,84 @@
             device_id_type=MESH,
         )
 
-    for k in range(chunks + 1):
-        if k < chunks:
-            load(k).wait()
-            for t in range(k * CHUNK, (k + 1) * CHUNK):
-                transform(t)
-        if k:
-            for t in range((k - 1) * CHUNK, k * CHUNK):
-                store(t)
-        if k * CHUNK == cut:
-            pl.semaphore_wait(barrier, neighbours + 2 * (nz - 1))
-            share_stats(0)
-    share_stats(1)
-    for g in range(2):
-        pair_copy(g).start()
-    greet(plane_sem)
+    def transform_all(x_sem, *accumulators):
+        products = accumulators[:2], accumulators[2:]
+
+        def load(k):
+            return pltpu.make_async_copy(
+                x_hbm.at[pl.ds(k * CHUNK, CHUNK)], x_buf.at[pl.ds(k * CHUNK, CHUNK)], x_sem.at[k]
+            )
+
+        @pl.loop(0, chunks)
+        def _(k):
+            load(k).start()
+
+        for dz in by_distance(nz):
+            for c in range(2):
+                if dz:
+                    pl.semaphore_signal(
+                        barrier,
+                        inc=1,
+                        device_id={"tmpl": 2 * chip + c, "grid": lax.rem(z + dz, nz)},
+                        device_id_type=MESH,
+                    )
+        greet(barrier)
+
+
+        fill_table(table, x_hbm.shape[3] // 2)
+
+        for unit in range(2):
+            for acc in products[unit]:
+                pltpu.matmul_pop(acc)
+            pltpu.matmul_push_rhs(table[...], staging_register=0, mxu_index=unit)
+
+        def transform(t):
+            for part in range(2):
+                operands = []
+                for parity in range(2):
+                    value = x_buf[t, :, pl.ds(parity, lines, stride=2), :].reshape(rows * lines, LANES)
+                    high = value.astype(jnp.bfloat16)
+                    if part:
+                        high = (value - high.astype(jnp.float32)).astype(jnp.bfloat16)
+                    operands.append(high)
+                pltpu.matmul_acc_lhs(
+                    products[t % 2][t // 2 % 2],
+                    jnp.concatenate(operands, axis=1),
+                    load_staged_rhs=0 if t < 2 and part == 0 else None,
+                )
+
+        def store(t):
+            product = pltpu.matmul_pop(products[t % 2][t // 2 % 2])
+            value = (product[:, :LANES] + product[:, LANES:]).reshape(rows, nx, 8, LANES)
+            for b in range(nx):
+                h, slot = places_of[b]
+                score[h, t, pl.ds(slot * rows, rows)] = value[:, b]
+            flat = value.reshape(rows * nx, 8, LANES)
+            part_sum[pl.ds(t, 1)] = jnp.sum(jnp.sum(flat, axis=0), axis=0, keepdims=True)
+            part_sq[pl.ds(t, 1)] = jnp.sum(jnp.sum(flat * flat, axis=0), axis=0, keepdims=True)
+
+        for k in range(chunks + 1):
+            if k < chunks:
+                load(k).wait()
+                for t in range(k * CHUNK, (k + 1) * CHUNK):
+                    transform(t)
+            if k:
+                for t in range((k - 1) * CHUNK, k * CHUNK):
+                    store(t)
+            if k * CHUNK == cut:
+                pl.semaphore_wait(barrier, neighbours + 2 * (nz - 1))
+                share_stats(0)
+        share_stats(1)
+        for g in range(2):
+            pair_copy(g).start()
+        greet(plane_sem)
+
+    wide = 2 * LANES
+    pl.run_scoped(
+        transform_all,
+        pltpu.SemaphoreType.DMA((chunks,)),
+        *(pltpu.ACC(n // 2)((wide, wide), jnp.float32) for n in range(4)),
+    )
 
     for g in range(2):
         norms(g)
@@ -354,8 +363,14 @@
         got[pl.ds(chip * piece, piece), :] = mine[pl.ds((8 + 2 * y) * piece, piece), :]
 
     all_stats(0, 2 * (slots - 1)).wait_send()
-    for g in range(2):
-        pair_copy(g).wait_send()
+    pltpu.make_async_remote_copy(
+        src_ref=score.at[1 - core],
+        dst_ref=other,
+        send_sem=pair_send,
+        recv_sem=pair_recv.at[0],
+        device_id={"tmpl": sibling, "grid": z},
+        device_id_type=MESH,
+    ).wait_send()
 
     def all_lists(number):
         return pltpu.make_async_remote_copy(
@@ -388,14 +403,6 @@
     out_ref[TOP] = total * (1.0 / math.sqrt(2 * targets * local))
 
 
-def scoped_kernel(sizes, *refs):
-    def run(*products):
-        kernel(sizes, *refs, (products[:2], products[2:]))
-
-    rows = 2 * LANES
-    pl.run_scoped(run, *(pltpu.ACC(n // 2)((rows, 2 * LANES), jnp.float32) for n in range(4)))
-
-
 def place_kernel(merged, best_ref, sum_ref):
     half = LANES // 2
     for j in range(2):
@@ -414,7 +421,7 @@
     targets = nx * ny
     dma = pltpu.SemaphoreType.DMA
     merged = pl.pallas_call(
-        functools.partial(scoped_kernel, sizes),
+        functools.partial(kernel, sizes),
         out_shape=jax.ShapeDtypeStruct((PARTS, rows, LANES), jnp.float32),
         in_specs=[pl.BlockSpec(memory_space=pltpu.HBM)],
         out_specs=pl.BlockSpec(memory_space=pltpu.VMEM),
@@ -431,8 +438,7 @@
             pltpu.VMEM((places, PARTS, 8, LANES), jnp.float32),
             pltpu.VMEM((targets * piece, LANES), jnp.float32),
             pltpu.VMEM((targets * piece, LANES), jnp.float32),
-            dma((local // CHUNK,)),
-            dma((2,)),
+            dma,
             dma((2,)),
             dma,
             dma((2,)),

time: 23.2 us -> 23.1 us (level)
  no operation moved by 1% of the time
where the time goes in v7:
time: 23.1 us; the launch traced here: 23 us
  Pallas kernels  22.3 us (97%)
  between operations  0.64 us (3%)
    pallas_call x1, Pallas kernels, body(): pl.pallas_call(functools.partial(kernel, sizes), out_shape=jax.ShapeDtype...  21.6 us
    pallas_call x1, Pallas kernels, body(): pl.pallas_call(place_kernel, out_shape=(jax.ShapeDtypeStruct((TOP, rows,...  0.72 us

profile of v7, /device:TPU:1, one launch (start us, length us, event | category | flops | bytes accessed | tf_op | source)
XLA Modules:
  0.0 23.0 jit_solution(16630909450927606694)
XLA Ops:
  0.6 21.6 %shard_map.30.merged = f32[5,8,128]{2,1,0:T(8,128)S(1)} custom-call(f32[32,8,64,128]{3,2,1,0:T(8,128)} %x_hbm.1), custom_call_target="tpu_custom_call" | custom-call | tf_op jit(solution)/shard_map/pallas_call | solution.py:423
  22.2 0.7 %shard_map.31 = (f32[4,8,2,64]{3,2,1,0:T(2,128)}, f32[8,2,64]{2,1,0:T(2,128)}) custom-call(f32[5,8,128]{2,1,0:T(8,128)S(1)} %shard_map.30.merged), custom_call_target="tpu_custom_call" | custom-call | tf_op jit(solution)/shard_map/pallas_call | solution.py:453

commit v8 on v7

--- a/solution.py
+++ b/solution.py
@@ -349,12 +349,12 @@
                             at = slot * (8 * piece) + (k * rows + low + p)
                             mine[pl.ds(at, 8, stride=piece), :] = parts[k]
                 own_column = (core == 0) & (slot == 1)
-                order = [(0, 1)] + [(k, c) for k in by_distance(ny) for c in range(2)]
+                order = [(0, 1)] * (turn == 0) + [(k, c) for k in by_distance(ny) for c in (1, 0)]
                 for n, (k, c) in enumerate(order):
-                    line = 1 if n == 0 else 2 * lax.rem(y + k, ny) + c
+                    line = 1 if n + turn == 0 else 2 * lax.rem(y + k, ny) + c
                     here = jnp.logical_not(own_column & (line == 2 * y + core))
 
-                    @pl.when(here & ((line != 1) if n else True))
+                    @pl.when(here & ((line != 1) if n and turn == 0 else True))
                     def _():
                         list_copy(slot, line).start()
 

time: 23.1 us -> 23.1 us (level)
  no operation moved by 1% of the time
where the time goes in v8:
time: 23.1 us; the launch traced here: 23 us
  Pallas kernels  22.3 us (97%)
  between operations  0.64 us (3%)
    pallas_call x1, Pallas kernels, body(): pl.pallas_call(functools.partial(kernel, sizes), out_shape=jax.ShapeDtype...  21.6 us
    pallas_call x1, Pallas kernels, body(): pl.pallas_call(place_kernel, out_shape=(jax.ShapeDtypeStruct((TOP, rows,...  0.72 us

profile of v8, /device:TPU:1, one launch (start us, length us, event | category | flops | bytes accessed | tf_op | source)
XLA Modules:
  0.0 23.0 jit_solution(6281734757589334636)
XLA Ops:
  0.6 21.6 %shard_map.30.merged = f32[5,8,128]{2,1,0:T(8,128)S(1)} custom-call(f32[32,8,64,128]{3,2,1,0:T(8,128)} %x_hbm.1), custom_call_target="tpu_custom_call" | custom-call | tf_op jit(solution)/shard_map/pallas_call | solution.py:423
  22.2 0.7 %shard_map.31 = (f32[4,8,2,64]{3,2,1,0:T(2,128)}, f32[8,2,64]{2,1,0:T(2,128)}) custom-call(f32[5,8,128]{2,1,0:T(8,128)S(1)} %shard_map.30.merged), custom_call_target="tpu_custom_call" | custom-call | tf_op jit(solution)/shard_map/pallas_call | solution.py:453
